TPU v7x, 32 devices: a whole 2x2x4 slice. The times are simulated.
32 devices in a mesh: grow: 4 (over y, x), gcol: 8 (over z, core).
Axes of the slice: x: 2, y: 2, z: 4, core: 2. Of those that a mesh axis runs over, the one named last changes fastest.
Arguments:
- psi: float32 [32768, 1024], P(('grow', 'gcol')), may hold values from -6 to 6
- vpsi: float32 [32768, 1024], P(('grow', 'gcol')), may hold values from -6 to 6
- kinetic: float32 [32768], P(('grow', 'gcol')), may hold values from 0.1 to 10
- mixing: float32 [1024, 1024], P('grow', 'gcol'), may hold values from -0.1875 to 0.1875
Outputs:
- residual: float32 [32768, 1024], P(('grow', 'gcol'))
- projected: float32 [1024, 1024], P('grow', 'gcol')
All inputs are finite; a program needn't handle non-finite values.
Results may differ from a plain program's by a relative error of at most 0.000073.
Values sent between devices are 32-bit elements; how exact they have to be, the bound alone decides.
No kernel may reach another device: no remote copies, remote signals or barrier semaphores. Data moves between devices by JAX's collectives and lax.ppermute only.
A program may use at most 128 MiB of HBM per device.

v0:
```python
import jax
import jax.numpy as jnp
from jax import lax
from jax.sharding import PartitionSpec as P


def body(psi, vpsi, kinetic, mixing):
    n_grow = lax.axis_size("grow")
    n_gcol = lax.axis_size("gcol")
    bands = psi.shape[1]
    scale = 1.0 / (psi.shape[0] * n_grow * n_gcol)
    hpsi = kinetic[:, None] * psi + vpsi
    block_rows = bands // n_grow
    block_cols = bands // n_gcol
    partial_value = (
        lax.dot_general(
            psi,
            hpsi,
            (((0,), (0,)), ((), ())),
            precision=lax.Precision.HIGHEST,
            preferred_element_type=jnp.float32,
        )
        * scale
    )
    full = lax.psum(partial_value, ("grow", "gcol"))
    row_start = lax.axis_index("grow") * block_rows
    col_start = lax.axis_index("gcol") * block_cols
    projected = lax.dynamic_slice(full, (row_start, col_start), (block_rows, block_cols))
    correction = hpsi - jnp.dot(
        psi, full, precision=lax.Precision.HIGHEST, preferred_element_type=jnp.float32
    )
    mix_panel = lax.all_gather(mixing, "gcol", axis=1, tiled=True)
    residual = jnp.dot(
        correction,
        lax.all_gather(mix_panel, "grow", axis=0, tiled=True),
        precision=lax.Precision.HIGHEST,
        preferred_element_type=jnp.float32,
    )
    return (residual, projected)


def solution(mesh):
    return jax.shard_map(
        body,
        mesh=mesh,
        in_specs=(
            P(("grow", "gcol"), None),
            P(("grow", "gcol"), None),
            P(("grow", "gcol")),
            P("grow", "gcol"),
        ),
        out_specs=(P(("grow", "gcol"), None), P("grow", "gcol")),
        check_vma=False,
    )
```

profile of v0, /device:TPU:0, one launch (start us, length us, event | category | flops | bytes accessed | tf_op | source)
XLA Modules:
  0.0 237.2 jit_solution(7438107211966366127)
XLA Ops:
  8.0 0.0 all-gather.3.cloned.1.call-start
  8.0 0.7 all-gather.3.cloned.1.call-update
  8.7 0.0 all-reduce.2.cloned.1.call-start
  8.8 18.8 %multiply_bitcast_fusion = f32[1024,1024]{0,1:T(8,128)} fusion(f32[1024,1024]{1,0:T(8,128)} %param.4, f32[1024,1024]{1,0:T(8,128)} %param.5, f32[1024]{0:T(1024)} %param.6), kind=kOutput, calls=%fused_computation.2 | convolution fusion | flops 12888047616 | bytes 12587008 | tf_op jit(solution)/shard_map/dot_general | solution.py:16
  27.5 0.0 all-reduce.2.cloned.1.call-update
  27.6 0.2 all-gather.5.cloned.1.call-start
  27.8 9.2 %all-gather.3.cloned.1.call-done = f32[256,1024]{1,0:T(8,128)} async-done(((f32[256,128]{1,0:T(8,128)}), f32[256,1024]{1,0:T(8,128)}) %all-gather.3.cloned.1.call-update) | async-done | bytes 1048592 | tf_op jit(solution)/shard_map/all_gather | solution.py:32
  37.0 0.0 all-gather.5.cloned.1.call-update
  37.1 154.0 %all-reduce.2.cloned.1.call-done = f32[1024,1024]{0,1:T(8,128)} async-done(((f32[1024,1024]{0,1:T(8,128)}), f32[1024,1024]{0,1:T(8,128)}) %all-reduce.2.cloned.1.call-update) | async-done | bytes 4194320 | tf_op jit(solution)/shard_map/psum | solution.py:25
  191.1 0.9 dynamic_slice.3
  192.0 0.8 copy.6
  192.7 0.0 copy-start
  192.7 17.7 %fusion.4 = f32[1024,1024]{0,1:T(8,128)} fusion(f32[1024,1024]{0,1:T(8,128)} %all-reduce.2.cloned.1.call-done, f32[1024,1024]{1,0:T(8,128)} %param.4), kind=kOutput, calls=%fused_computation.7 | convolution fusion | flops 12884901888 | bytes 12582912 | tf_op jit(solution)/shard_map/dot_general | solution.py:29
  210.5 0.0 all-gather.5.cloned.1.call-done
  210.5 0.0 copy-done
  210.5 19.3 %fusion = f32[1024,1024]{1,0:T(8,128)} fusion(f32[1024,1024]{1,0:T(8,128)} %all-gather.5.cloned.1.call-done, f32[1024,1024]{0,1:T(8,128)} %fusion.4, f32[1024,1024]{1,0:T(8,128)} %param.5, f32[1024,1024]{1,0:T(8,128)} %param.4, f32[1024]{0:T(1024)S(1)} %copy-done), kind=kOutput, calls=%fused_computation.1 | convolution fusion | flops 12888047616 | bytes 20975616 | tf_op jit(solution)/shard_map/dot_general | solution.py:33
Async XLA Ops:
  8.0 29.0 %all-gather.3.cloned.1.call-start = ((), (), s32[]{:S(2)}) async-start(), calls=%async_computation.1 | async-start | bytes 1179648 | tf_op jit(solution)/shard_map/all_gather | solution.py:32
  8.7 182.3 %all-reduce.2.cloned.1.call-start = ((), (), s32[]{:S(2)}) async-start(), calls=%async_computation | async-start | bytes 8388608 | tf_op jit(solution)/shard_map/psum | solution.py:25
  27.6 182.9 %all-gather.5.cloned.1.call-start = ((), (), s32[]{:S(2)}) async-start(), calls=%async_computation.2 | async-start | bytes 5242880 | tf_op jit(solution)/shard_map/all_gather | solution.py:35
  192.7 17.7 %copy-start = (f32[1024]{0:T(1024)S(1)}, f32[1024]{0:T(1024)}, u32[]{:S(2)}) copy-start(f32[1024]{0:T(1024)} %param.6) | copy-start | bytes 12292
Sparse Core Ops, SparseCore 0:
  10.4 26.6 all-gather.2
  38.9 52.5 all-gather.4
Sparse Core Ops, SparseCore 1:
  27.6 163.4 all-reduce.1
where the time goes:
time: 237 us
  waiting for transfers between devices  164 us (69%)
  matrix products  55.8 us (24%)
  between operations  15.5 us (7%)
    psum x1, waiting for transfers between devices, body(): full = lax.psum(partial_value, ('grow', 'gcol'))  154 us
    dot_general x1, matrix products, body(): jnp.dot(correction, lax.all_gather(mix_panel, 'grow', axis=0, tiled=True)...  19.3 us
    dot_general x1, matrix products, body(): lax.dot_general(psi, hpsi, (((0,), (0,)), ((), ())), precision=lax.Precis...  18.8 us
    dot_general x1, matrix products, body(): jnp.dot(psi, full, precision=lax.Precision.HIGHEST, preferred_element_typ...  17.7 us
    all_gather x1, waiting for transfers between devices, body(): mix_panel = lax.all_gather(mixing, 'gcol', axis=1, tiled=True)  9.25 us
  transfers between devices with their start and end apart: 3, of which 2 were waited for; matrix products, arithmetic and copies ran while one was open for 16% of the time, Pallas kernels for 0%

commit v1 on v0

v1 whole, which is shorter than its diff:
```python
import functools

import jax
import jax.numpy as jnp
from jax import lax
from jax.experimental import pallas as pl
from jax.experimental.pallas import tpu as pltpu
from jax.sharding import PartitionSpec as P


F32, BF16 = jnp.float32, jnp.bfloat16
CHAINS = 2


def split(x):
    high = x.astype(BF16)
    return high, (x - high.astype(F32)).astype(BF16)


def mm(a, b, dims=((1,), (0,))):
    return lax.dot_general(a, b, (dims, ((), ())), preferred_element_type=F32)


def mm3(a, b):
    (ah, al), (bh, bl) = a, b
    return mm(ah, bh) + (mm(al, bh) + mm(ah, bl))


def cost(flops, nbytes):
    return pl.CostEstimate(flops=flops, bytes_accessed=nbytes, transcendentals=0)


def params(mib):
    return pltpu.CompilerParams(dimension_semantics=("arbitrary",), vmem_limit_bytes=mib << 20)


def column(x):
    n, lanes = x.shape
    eye = lax.broadcasted_iota(jnp.int32, (lanes, lanes), 0) == lax.broadcasted_iota(jnp.int32, (lanes, lanes), 1)
    return jnp.concatenate([jnp.sum(jnp.where(eye, x[i : i + 1], 0.0), 1, keepdims=True) for i in range(n)], 0)


def share_kernel(dims, scale, core_ref, psi_ref, vpsi_ref, kin_ref, *rest):
    G, Z, b, bc = dims
    outs, (ph_ref, pl_ref, hh_ref, hl_ref, acc) = rest[: 2 * CHAINS], rest[2 * CHAINS :]
    r = pl.program_id(0)
    psi = psi_ref[...]
    h = column(kin_ref[0]) * psi + vpsi_ref[...]
    ph, pl_ = split(psi)
    hh, hl = split(h)
    hh_ref[...], hl_ref[...] = hh, hl
    for k in range(CHAINS):
        for g in range(G):
            to, at = slice(g * b, (g + 1) * b), slice((g * CHAINS + k) * b, (g * CHAINS + k + 1) * b)
            ph_ref[k, :, to], pl_ref[k, :, to] = ph[:, at], pl_[:, at]
    pht = ph.T
    left = jnp.concatenate([pht, pl_.T, pht], 1)
    right = jnp.concatenate([hh, hh, hl], 0)
    n = psi.shape[1]
    t = 256

    @pl.when(r == 0)
    def _():
        for j in range(n // t):
            acc[:, j * t : (j + 1) * t] = mm(left, right[:, j * t : (j + 1) * t])

    @pl.when(r > 0)
    def _():
        for j in range(n // t):
            acc[:, j * t : (j + 1) * t] += mm(left, right[:, j * t : (j + 1) * t])

    @pl.when(r == pl.num_programs(0) - 1)
    def _():
        core = core_ref[0]
        half = n // 2
        br = n // G
        for side, c in enumerate((core, 1 - core)):
            cols = pl.ds(pl.multiple_of(c * half, half), half)
            for k in range(CHAINS):
                out = outs[2 * k + side]
                for g in range(G):
                    x = acc[g * br + k * b : g * br + (k + 1) * b, cols] * scale
                    for z in range(Z):
                        out[g, z] = x[:, z * bc : (z + 1) * bc]


def share(core, psi, vpsi, kin, dims, scale):
    G, _, b, _ = dims
    rows, bands = psi.shape
    t = 256
    blk = pl.BlockSpec((t, bands), lambda i, c: (i, 0))
    whole = pl.BlockSpec(dims, lambda i, c: (0, 0, 0, 0))
    chain = pl.BlockSpec((CHAINS, t, G * b), lambda i, c: (0, i, 0))
    return pl.pallas_call(
        functools.partial(share_kernel, dims, scale),
        grid_spec=pltpu.PrefetchScalarGridSpec(
            num_scalar_prefetch=1,
            grid=(rows // t,),
            in_specs=[blk, blk, pl.BlockSpec((1, t // 128, 128), lambda i, c: (i, 0, 0))],
            out_specs=[whole] * (2 * CHAINS) + [chain] * 2 + [blk] * 2,
            scratch_shapes=[pltpu.VMEM((bands, bands), F32)],
        ),
        out_shape=[jax.ShapeDtypeStruct(dims, F32)] * (2 * CHAINS)
        + [pltpu.HBM((CHAINS, rows, G * b), BF16)] * 2
        + [pltpu.HBM((rows, bands), BF16)] * 2,
        compiler_params=params(26),
        cost_estimate=cost(6 * rows * bands * bands, 12 * rows * bands),
        name="share",
    )(core, *(pltpu.with_memory_space_constraint(x, pltpu.HBM) for x in (psi, vpsi)), kin.reshape(rows // t, t // 128, 128))


def joined_kernel(core_ref, own_ref, sib_ref, high_ref, low_ref):
    G, Z, br, bc = own_ref.shape
    core = core_ref[0]
    for c, ref in ((core, own_ref), (1 - core, sib_ref)):
        for g in range(G):
            for z in range(Z):
                at = slice(g * br, (g + 1) * br), pl.ds(pl.multiple_of((2 * z + c) * bc, bc), bc)
                high_ref[at], low_ref[at] = split(ref[g, z])


def joined(core, own, sib):
    G, _, br, bc = own.shape
    bands = G * br
    if bc % 128:
        return split(ordered(own, sib, core[0], 2).transpose(0, 3, 1, 2, 4).reshape(bands, bands))
    whole = pl.BlockSpec(own.shape, lambda i, c: (0, 0, 0, 0))
    return pl.pallas_call(
        joined_kernel,
        grid_spec=pltpu.PrefetchScalarGridSpec(
            num_scalar_prefetch=1,
            grid=(1,),
            in_specs=[whole, whole],
            out_specs=[pl.BlockSpec((bands, bands), lambda i, c: (0, 0))] * 2,
        ),
        out_shape=[jax.ShapeDtypeStruct((bands, bands), BF16)] * 2,
        compiler_params=params(14),
        cost_estimate=cost(100 * bands * bands, 12 * bands * bands),
        name="joined",
    )(core, own, sib)


def mixed_kernel(hh_ref, hl_ref, mh_ref, ml_ref, out_ref):
    n = mh_ref.shape[1]
    for j in range(n // 512):
        s = slice(j * 512, (j + 1) * 512)
        out_ref[:, s] = mm3((hh_ref[...], hl_ref[...]), (mh_ref[:, s], ml_ref[:, s]))


def mixed(h, m):
    rows, bands = h[0].shape
    t = 256
    blk = pl.BlockSpec((t, bands), lambda i: (i, 0))
    return pl.pallas_call(
        mixed_kernel,
        grid=(rows // t,),
        in_specs=[blk, blk] + [pl.BlockSpec((bands, bands), lambda i: (0, 0))] * 2,
        out_specs=blk,
        out_shape=jax.ShapeDtypeStruct((rows, bands), F32),
        compiler_params=params(14),
        cost_estimate=cost(6 * rows * bands * bands, 16 * rows * bands),
        name="mixed",
    )(*h, *m)


def turned_kernel(core_ref, own_ref, sib_ref, m1h, m1l, m2h, m2l, out_ref):
    out_ref[...] = mm3(split(own_ref[...]), (m1h[...], m1l[...])) + mm3(split(sib_ref[...]), (m2h[...], m2l[...]))


def turned(core, own, sib, m):
    b, half = own.shape
    row = pl.BlockSpec((b, half), lambda i, c: (0, 0))
    m1 = pl.BlockSpec((half, half), lambda i, c: (c[0], c[0]))
    m2 = pl.BlockSpec((half, half), lambda i, c: (1 - c[0], c[0]))
    return pl.pallas_call(
        turned_kernel,
        grid_spec=pltpu.PrefetchScalarGridSpec(
            num_scalar_prefetch=1, grid=(1,), in_specs=[row, row, m1, m1, m2, m2], out_specs=row
        ),
        out_shape=jax.ShapeDtypeStruct((b, half), F32),
        compiler_params=params(8),
        cost_estimate=cost(12 * b * half * half, 8 * half * half),
        name="turned",
    )(core, own, sib, *m, *m)


def less_kernel(core_ref, acc_ref, ph_ref, pl_ref, own_ref, sib_ref, out_ref, wh, wl):
    n = own_ref.shape[1]
    core = core_ref[0]

    @pl.when(pl.program_id(0) == 0)
    def _():
        wh[0], wl[0] = split(own_ref[...])
        wh[1], wl[1] = split(sib_ref[...])

    for j in range(2):
        s = pl.ds(pl.multiple_of(jnp.where(core == j, 0, 1) * n, n), n)
        out_ref[:, s] = acc_ref[:, s] - mm3((ph_ref[...], pl_ref[...]), (wh[j], wl[j]))


def less(core, acc, psi, own, sib, k):
    rows, bands = acc.shape
    kk, half = own.shape
    t = 256
    blk = pl.BlockSpec((t, bands), lambda i, c: (i, 0))
    part = pl.BlockSpec((None, t, kk), lambda i, c: (k, i, 0))
    w = pl.BlockSpec((kk, half), lambda i, c: (0, 0))
    return pl.pallas_call(
        less_kernel,
        grid_spec=pltpu.PrefetchScalarGridSpec(
            num_scalar_prefetch=1,
            grid=(rows // t,),
            in_specs=[blk, part, part, w, w],
            out_specs=blk,
            scratch_shapes=[pltpu.VMEM((2, kk, half), BF16)] * 2,
        ),
        out_shape=jax.ShapeDtypeStruct((rows, bands), F32),
        compiler_params=params(14),
        cost_estimate=cost(6 * rows * kk * bands, 16 * rows * bands),
        name="less",
    )(core, acc, *psi, own, sib)


def pick(x, i, axis):
    return lax.dynamic_index_in_dim(x, i, axis, keepdims=False)


def hop(x, axis, mask):
    n = lax.axis_size(axis)
    return lax.ppermute(x, axis, [(i, i ^ mask) for i in range(n)])


def bit_of(axis, mask):
    return jnp.where((lax.axis_index(axis) & mask) != 0, 1, 0)


def ordered(mine, theirs, bit, axis):
    low = bit == 0
    return jnp.stack([jnp.where(low, mine, theirs), jnp.where(low, theirs, mine)], axis)


def scatter(x, bits, order):
    bits = list(bits)
    for bit in order:
        a = bits.index(bit)
        mine = bit_of(*bit)
        x = pick(x, mine, a) + hop(pick(x, 1 - mine, a), *bit)
        bits.remove(bit)
    return x


def gather(x, bits, order, have=()):
    have = list(have)
    for bit in order:
        a = sum(bits.index(other) < bits.index(bit) for other in have)
        x = ordered(x, hop(x, *bit), bit_of(*bit), a)
        have.append(bit)
    return x


def after(x, *others):
    return lax.optimization_barrier((x, *others))[0]


def axis_bits(axis, low):
    n = lax.axis_size(axis)
    return [(axis, 1 << i) for i in range(low, n.bit_length() - 1)][::-1]


def body(psi, vpsi, kinetic, mixing):
    G, C = lax.axis_size("grow"), lax.axis_size("gcol")
    rows, bands = psi.shape
    Z = C // 2
    br, bc, half = bands // G, bands // C, bands // 2
    b = br // CHAINS
    gb, zb = axis_bits("grow", 0), axis_bits("gcol", 1)
    up = gb[::-1]
    core = lax.axis_index("gcol") % 2
    core1 = core.reshape(1)

    *pieces, ph, pl_, hh, hl = share(core1, psi, vpsi, kinetic, (G, Z, b, bc), 1.0 / (rows * G * C))

    m = gather(after(mixing, pieces[0]), zb, zb)
    ma = gather(m[..., : br // 2, :], gb, up).reshape(G, Z, br // 2, bc)
    mb = gather(m[..., br // 2 :, :], gb, gb).reshape(G, Z, br // 2, bc)
    m_own = jnp.concatenate([ma, mb], 2)
    m_all = joined(core1, m_own, hop(m_own, "gcol", 1))
    acc = mixed((hh, hl), m_all)

    h_parts = []
    for k in range(CHAINS):
        there, back = (up, gb) if k % 2 == 0 else (gb, up)
        q = pieces[2 * k] + hop(pieces[2 * k + 1], "gcol", 1)
        q = q.reshape((2,) * (len(gb) + len(zb)) + (b, bc))
        q = scatter(q, gb + zb, there + zb[:0:-1])
        q = q + hop(q, *zb[0])
        h_parts.append(pick(q, bit_of(*zb[0]), 0))
        row = gather(q, zb, zb[1:], zb[:1]).reshape(Z, b, bc).transpose(1, 0, 2).reshape(b, half)
        w = turned(core1, row, hop(row, "gcol", 1), m_all)
        w = gather(w, gb, back).reshape(G * b, half)
        acc = less(core1, acc, (ph, pl_), w, hop(w, "gcol", 1), k)

    h = jnp.concatenate(h_parts, 0)
    projected = lax.ppermute(h, "gcol", [(i, (i % 2) * Z + i // 2) for i in range(C)])
    return acc, projected


def solution(mesh):
    return jax.shard_map(
        body,
        mesh=mesh,
        in_specs=(
            P(("grow", "gcol"), None),
            P(("grow", "gcol"), None),
            P(("grow", "gcol")),
            P("grow", "gcol"),
        ),
        out_specs=(P(("grow", "gcol"), None), P("grow", "gcol")),
        check_vma=False,
    )
```

time: 237 us -> 152 us (0.64)
  the two profiles are of different devices: /device:TPU:0 before, /device:TPU:1 now
where the time goes in v1:
time: 152 us
  waiting for transfers between devices  56.6 us (37%)
  starting transfers between devices  50.5 us (33%)
  Pallas kernels  32.1 us (21%)
  other arithmetic  8.59 us (6%)
  local copies, waits for them, and re-layouts  2.8 us (2%)
    ppermute x27, waiting for transfers between devices, hop(): return lax.ppermute(x, axis, [(i, i ^ mask) for i in range(n)])  54.3 us
    ppermute x27, starting transfers between devices, hop(): return lax.ppermute(x, axis, [(i, i ^ mask) for i in range(n)])  46.5 us
    pallas_call x1, Pallas kernels, share(): pl.pallas_call(functools.partial(share_kernel, dims, scale), grid_spec=pl...  13.1 us
    pallas_call x2, Pallas kernels, less(): pl.pallas_call(less_kernel, grid_spec=pltpu.PrefetchScalarGridSpec(num_sc...  9.48 us
    pallas_call x1, Pallas kernels, mixed(): pl.pallas_call(mixed_kernel, grid=(rows // t,), in_specs=[blk, blk] + [pl...  7.27 us
    another operation x24, other arithmetic, ordered(): jnp.stack([jnp.where(low, mine, theirs), jnp.where(low, theirs, mine)], a...  5.47 us
    ppermute x1, starting transfers between devices, body(): lax.ppermute(h, 'gcol', [(i, i % 2 * Z + i // 2) for i in range(C)])  3.98 us
  transfers between devices with their start and end apart: 28, of which 15 were waited for; matrix products, arithmetic and copies ran while one was open for 5% of the time, Pallas kernels for 9%

profile of v1, /device:TPU:1, one launch (start us, length us, event | category | flops | bytes accessed | tf_op | source)
XLA Modules:
  0.0 151.6 jit_solution(3274732020070384234)
XLA Ops:
  1.3 13.1 %share.1 = (f32[4,4,128,128]{3,2,1,0:T(8,128)S(1)}, f32[4,4,128,128]{3,2,1,0:T(8,128)S(1)}, f32[4,4,128,128]{3,2,1,0:T(8,128)S(1)}, f32[4,4,128,128]{3,2,1,0:T(8...) custom-call(s32[1]{0:T(128)} %bitcast.core_ref, ...), custom_call_target="tpu_custom_call" | custom-call | flops 6442450944 | bytes 12582912 | tf_op jit(solution)/shard_map/share/pallas_call | solution.py:94
  15.4 3.1 %collective-permute-start = (f32[256,128]{1,0:T(8,128)S(1)}, f32[256,128]{1,0:T(8,128)}, u32[]{:S(2)}, u32[]{:S(2)}) collective-permute-start(f32[256,128]{1,0:T(8,128)S(1)} %copy-done.6), channel_id=1, source_target_pairs={{0,4},{1,5},{2,6},{3,7},{4,0},{5,1},{6,2},{7,3},{8,12},{9,13},{10,... | collective-permute-start | bytes 393224 | tf_op jit(solution)/shard_map/ppermute | solution.py:230
  18.5 6.1 %collective-permute-done = f32[256,128]{1,0:T(8,128)} collective-permute-done((f32[256,128]{1,0:T(8,128)S(1)}, f32[256,128]{1,0:T(8,128)}, u32[]{:S(2)}, u32[]{:S(2)}) %collective-permute-start) | collective-permute-done | bytes 131104 | tf_op jit(solution)/shard_map/ppermute | solution.py:230
  28.1 5.0 %collective-permute-done.1 = f32[2,256,128]{2,1,0:T(8,128)} collective-permute-done((f32[2,256,128]{2,1,0:T(8,128)}, f32[2,256,128]{2,1,0:T(8,128)}, u32[]{:S(2)}, u32[]{:S(2)}) %collective-permute-start.1) | collective-permute-done | bytes 262176 | tf_op jit(solution)/shard_map/ppermute | solution.py:230
  35.8 2.5 %collective-permute-start.17 = (f32[4,4,128,128]{3,2,1,0:T(8,128)S(1)}, f32[4,4,128,128]{3,2,1,0:T(8,128)}, u32[]{:S(2)}, u32[]{:S(2)}) collective-permute-start(f32[4,4,128,128]{3,2,1,0:T(8,128)S(1)} %get-tuple-element.23), channel_id=1, source_target_pairs={{0,1},{1,0},{2,3},{3,2},{4,5},{5,4},{6,7},{7,6},{8,9},{9,8},{10,11... | collective-permute-start | bytes 3145736 | tf_op jit(solution)/shard_map/ppermute | solution.py:230
  42.9 3.3 %collective-permute-done.4 = f32[2,2,128,128]{3,2,0,1:T(8,128)S(1)} collective-permute-done((f32[2,2,128,128]{3,2,0,1:T(8,128)S(1)}, f32[2,2,128,128]{3,2,0,1:T(8,128)S(1)}, u32[]{:S(2)}, u32[]{:S(2)}) %collective-permute-start.4) | collective-permute-done | bytes 262176 | tf_op jit(solution)/shard_map/ppermute | solution.py:230
  52.0 4.3 %collective-permute-done.3 = f32[2,2,2,128,128]{4,3,1,2,0:T(8,128)S(1)} collective-permute-done((f32[2,2,2,128,128]{4,3,1,2,0:T(8,128)S(1)}, f32[2,2,2,128,128]{4,3,1,2,0:T(8,128)S(1)}, u32[]{:S(2)}, u32[]{:S(2)}) %collective-permute-start.3) | collective-permute-done | bytes 524320 | tf_op jit(solution)/shard_map/ppermute | solution.py:230
  56.5 2.0 %collective-permute-done.5 = f32[2,2,2,128,128]{4,3,1,2,0:T(8,128)S(1)} collective-permute-done((f32[2,2,2,128,128]{4,3,1,2,0:T(8,128)S(1)}, f32[2,2,2,128,128]{4,3,1,2,0:T(8,128)S(1)}, u32[]{:S(2)}, u32[]{:S(2)}) %collective-permute-start.5) | collective-permute-done | bytes 524320 | tf_op jit(solution)/shard_map/ppermute | solution.py:230
  59.0 4.0 %collective-permute-start.6 = (f32[4,4,256,128]{3,2,1,0:T(8,128)S(1)}, f32[4,4,256,128]{3,2,1,0:T(8,128)S(1)}, u32[]{:S(2)}, u32[]{:S(2)}) collective-permute-start(f32[4,4,256,128]{3,2,1,0:T(8,128)S(1)} %pad_maximum_fusion.own_ref), channel_id=1, source_target_pairs={{0,1},{1,0},{2,3},{3,2},{4,5},{5,4},{6,7},{7,6},{8,9},{9,8},{10,11... | collective-permute-start | bytes 6291464 | tf_op jit(solution)/shard_map/ppermute | solution.py:230
  63.0 6.8 %collective-permute-done.8 = f32[2,2,2,128,128]{4,3,2,1,0:T(8,128)S(1)} collective-permute-done((f32[2,2,2,128,128]{4,3,2,1,0:T(8,128)S(1)}, f32[2,2,2,128,128]{4,3,2,1,0:T(8,128)S(1)}, u32[]{:S(2)}, u32[]{:S(2)}) %collective-permute-start.8) | collective-permute-done | bytes 524320 | tf_op jit(solution)/shard_map/ppermute | solution.py:230
  71.6 4.0 %collective-permute-done.9 = f32[2,2,128,128]{3,2,1,0:T(8,128)S(1)} collective-permute-done((f32[2,2,128,128]{3,2,1,0:T(8,128)S(1)}, f32[2,2,128,128]{3,2,1,0:T(8,128)S(1)}, u32[]{:S(2)}, u32[]{:S(2)}) %collective-permute-start.9) | collective-permute-done | bytes 262176 | tf_op jit(solution)/shard_map/ppermute | solution.py:230
  79.8 3.5 %collective-permute-start.11 = (f32[2,128,128]{2,1,0:T(8,128)S(1)}, f32[2,128,128]{2,1,0:T(8,128)S(1)}, u32[]{:S(2)}, u32[]{:S(2)}) collective-permute-start(f32[2,128,128]{2,1,0:T(8,128)S(1)} %bitcast_add_fusion.5), channel_id=1, source_target_pairs={{0,4},{1,5},{2,6},{3,7},{4,0},{5,1},{6,2},{7,3},{8,12},{9,13},{10,... | collective-permute-start | bytes 393224 | tf_op jit(solution)/shard_map/ppermute | solution.py:230
  86.2 3.0 %collective-permute-start.12 = (f32[2,128,128]{2,1,0:T(8,128)S(1)}, f32[2,128,128]{2,1,0:T(8,128)S(1)}, u32[]{:S(2)}, u32[]{:S(2)}) collective-permute-start(f32[2,128,128]{2,1,0:T(8,128)S(1)} %add.70), channel_id=1, source_target_pairs={{0,2},{1,3},{2,0},{3,1},{4,6},{5,7},{6,4},{7,5},{8,10},{9,11},{10,... | collective-permute-start | bytes 393224 | tf_op jit(solution)/shard_map/ppermute | solution.py:230
  89.9 3.1 %collective-permute-start.22 = (f32[2,128,128]{2,1,0:T(8,128)S(1)}, f32[2,128,128]{2,1,0:T(8,128)S(1)}, u32[]{:S(2)}, u32[]{:S(2)}) collective-permute-start(f32[2,128,128]{2,1,0:T(8,128)S(1)} %add.75), channel_id=1, source_target_pairs={{0,2},{1,3},{2,0},{3,1},{4,6},{5,7},{6,4},{7,5},{8,10},{9,11},{10,... | collective-permute-start | bytes 393224 | tf_op jit(solution)/shard_map/ppermute | solution.py:230
  93.1 6.8 %collective-permute-start.13 = (f32[128,512]{1,0:T(8,128)S(1)}, f32[128,512]{1,0:T(8,128)S(1)}, u32[]{:S(2)}, u32[]{:S(2)}) collective-permute-start(f32[128,512]{1,0:T(8,128)S(1)} %bitcast.102), channel_id=1, source_target_pairs={{0,1},{1,0},{2,3},{3,2},{4,5},{5,4},{6,7},{7,6},{8,9},{9,8},{10,11... | collective-permute-start | bytes 786440 | tf_op jit(solution)/shard_map/ppermute | solution.py:230
  99.9 1.7 %collective-permute-start.23 = (f32[128,512]{1,0:T(8,128)S(1)}, f32[128,512]{1,0:T(8,128)S(1)}, u32[]{:S(2)}, u32[]{:S(2)}) collective-permute-start(f32[128,512]{1,0:T(8,128)S(1)} %bitcast.104), channel_id=1, source_target_pairs={{0,1},{1,0},{2,3},{3,2},{4,5},{5,4},{6,7},{7,6},{8,9},{9,8},{10,11... | collective-permute-start | bytes 786440 | tf_op jit(solution)/shard_map/ppermute | solution.py:230
  105.7 5.6 %collective-permute-done.14 = f32[128,512]{1,0:T(8,128)S(1)} collective-permute-done((f32[128,512]{1,0:T(8,128)S(1)}, f32[128,512]{1,0:T(8,128)S(1)}, u32[]{:S(2)}, u32[]{:S(2)}) %collective-permute-start.14) | collective-permute-done | bytes 262176 | tf_op jit(solution)/shard_map/ppermute | solution.py:230
  113.3 10.7 %collective-permute-done.15 = f32[2,128,512]{2,1,0:T(8,128)S(1)} collective-permute-done((f32[2,128,512]{2,1,0:T(8,128)S(1)}, f32[2,128,512]{2,1,0:T(8,128)S(1)}, u32[]{:S(2)}, u32[]{:S(2)}) %collective-permute-start.15) | collective-permute-done | bytes 524320 | tf_op jit(solution)/shard_map/ppermute | solution.py:230
  124.3 1.8 %collective-permute-start.16 = (f32[512,512]{1,0:T(8,128)S(1)}, f32[512,512]{1,0:T(8,128)S(1)}, u32[]{:S(2)}, u32[]{:S(2)}) collective-permute-start(f32[512,512]{1,0:T(8,128)S(1)} %bitcast.98), channel_id=1, source_target_pairs={{0,1},{1,0},{2,3},{3,2},{4,5},{5,4},{6,7},{7,6},{8,9},{9,8},{10,11... | collective-permute-start | bytes 3145736 | tf_op jit(solution)/shard_map/ppermute | solution.py:230
  127.9 4.0 %collective-permute-start.27 = (f32[256,128]{1,0:T(8,128)S(1)}, f32[256,128]{1,0:T(8,128)S(1)}, u32[]{:S(2)}, u32[]{:S(2)}) collective-permute-start(f32[256,128]{1,0:T(8,128)S(1)} %pad_maximum_fusion.13), channel_id=1, source_target_pairs={{0,0},{1,4},{2,1},{3,5},{4,2},{5,6},{6,3},{7,7},{8,8},{9,12},{10,9... | collective-permute-start | bytes 393224 | tf_op jit(solution)/shard_map/ppermute | solution.py:304
  131.8 2.3 %collective-permute-done.27 = f32[256,128]{1,0:T(8,128)S(1)} collective-permute-done((f32[256,128]{1,0:T(8,128)S(1)}, f32[256,128]{1,0:T(8,128)S(1)}, u32[]{:S(2)}, u32[]{:S(2)}) %collective-permute-start.27) | collective-permute-done | bytes 131104 | tf_op jit(solution)/shard_map/ppermute | solution.py:304
  134.2 7.3 %mixed.1.acc_ref = f32[1024,1024]{1,0:T(8,128)S(1)} custom-call(bf16[1024,1024]{1,0:T(8,128)(2,1)S(1)} %copy-done.4, bf16[1024,1024]{1,0:T(8,128)(2,1)S(1)} %copy-done.5, bf16[1024,1024]{1,0:T(8,128)(2,1)S(1)} %get-tuple-element.17.mh_ref.m1h.m2h, bf16[1024,1024]{1,0:T(8,128)(2,1)S(1)} %get-tuple-element.18.ml_ref.m1l.m2l), custom_call_target="tpu_custom_call" | custom-call | flops 6442450944 | bytes 16777216 | tf_op jit(solution)/shard_map/mixed/pallas_call | solution.py:154
  141.5 4.2 %less.2.acc_ref = f32[1024,1024]{1,0:T(8,128)S(1)} custom-call(s32[1]{0:T(128)} %bitcast.core_ref, f32[1024,1024]{1,0:T(8,128)S(1)} %mixed.1.acc_ref, bf16[2,1024,512]{2,1,0:T(8,128)(2,1)S(1)} %copy-done, bf16[2,1024,512]{2,1,0:T(8,128)(2,1)S(1)} %copy-done.1, f32[512,512]{1,0:T(8,128)S(1)} %bitcast.99, f32[512,512]{1,0:T(8,128)S(1)} %collective-permute-done.16.sib_ref), custom_call_target="tpu_custom_call" | custom-call | flops 3221225472 | bytes 16777216 | tf_op jit(solution)/shard_map/less/pallas_call | solution.py:208
  145.7 5.2 %less.3 = f32[1024,1024]{1,0:T(8,128)} custom-call(s32[1]{0:T(128)} %bitcast.core_ref, f32[1024,1024]{1,0:T(8,128)S(1)} %less.2.acc_ref, bf16[2,1024,512]{2,1,0:T(8,128)(2,1)S(1)} %copy-done, bf16[2,1024,512]{2,1,0:T(8,128)(2,1)S(1)} %copy-done.1, f32[512,512]{1,0:T(8,128)S(1)} %bitcast.101, f32[512,512]{1,0:T(8,128)S(1)} %collective-permute-done.26.sib_ref), custom_call_target="tpu_custom_call" | custom-call | flops 3221225472 | bytes 16777216 | tf_op jit(solution)/shard_map/less/pallas_call | solution.py:208
  (105 shorter events, 37.2 us)
Async XLA Ops:
  15.4 9.2 %collective-permute-start = (f32[256,128]{1,0:T(8,128)S(1)}, f32[256,128]{1,0:T(8,128)}, u32[]{:S(2)}, u32[]{:S(2)}) collective-permute-start(f32[256,128]{1,0:T(8,128)S(1)} %copy-done.6), channel_id=1, source_target_pairs={{0,4},{1,5},{2,6},{3,7},{4,0},{5,1},{6,2},{7,3},{8,12},{9,13},{10,... | collective-permute-start | bytes 393224 | tf_op jit(solution)/shard_map/ppermute | solution.py:230
  26.3 6.9 %collective-permute-start.1 = (f32[2,256,128]{2,1,0:T(8,128)}, f32[2,256,128]{2,1,0:T(8,128)}, u32[]{:S(2)}, u32[]{:S(2)}) collective-permute-start(f32[2,256,128]{2,1,0:T(8,128)} %pad_maximum_fusion.10), channel_id=1, source_target_pairs={{0,2},{1,3},{2,0},{3,1},{4,6},{5,7},{6,4},{7,5},{8,10},{9,11},{10,... | collective-permute-start | bytes 786440 | tf_op jit(solution)/shard_map/ppermute | solution.py:230
  27.4 19.4 %collective-permute-start.7 = (f32[4,4,128,128]{3,2,1,0:T(8,128)}, f32[4,4,128,128]{3,2,1,0:T(8,128)}, u32[]{:S(2)}, u32[]{:S(2)}) collective-permute-start(f32[4,4,128,128]{3,2,1,0:T(8,128)} %copy-done.2), channel_id=1, source_target_pairs={{0,1},{1,0},{2,3},{3,2},{4,5},{5,4},{6,7},{7,6},{8,9},{9,8},{10,11... | collective-permute-start | bytes 3145736 | tf_op jit(solution)/shard_map/ppermute | solution.py:230
  34.9 6.1 %collective-permute-start.2 = (f32[2,2,128,128]{3,2,0,1:T(8,128)}, f32[2,2,128,128]{3,2,0,1:T(8,128)}, u32[]{:S(2)}, u32[]{:S(2)}) collective-permute-start(f32[2,2,128,128]{3,2,0,1:T(8,128)} %get-tuple-element.38), channel_id=1, source_target_pairs={{0,8},{8,0},{16,24},{24,16},{1,9},{9,1},{17,25},{25,17},{2,10},{10... | collective-permute-start | bytes 786440 | tf_op jit(solution)/shard_map/ppermute | solution.py:230
  35.8 13.5 %collective-permute-start.17 = (f32[4,4,128,128]{3,2,1,0:T(8,128)S(1)}, f32[4,4,128,128]{3,2,1,0:T(8,128)}, u32[]{:S(2)}, u32[]{:S(2)}) collective-permute-start(f32[4,4,128,128]{3,2,1,0:T(8,128)S(1)} %get-tuple-element.23), channel_id=1, source_target_pairs={{0,1},{1,0},{2,3},{3,2},{4,5},{5,4},{6,7},{7,6},{8,9},{9,8},{10,11... | collective-permute-start | bytes 3145736 | tf_op jit(solution)/shard_map/ppermute | solution.py:230
  38.3 7.9 %collective-permute-start.4 = (f32[2,2,128,128]{3,2,0,1:T(8,128)S(1)}, f32[2,2,128,128]{3,2,0,1:T(8,128)S(1)}, u32[]{:S(2)}, u32[]{:S(2)}) collective-permute-start(f32[2,2,128,128]{3,2,0,1:T(8,128)S(1)} %get-tuple-element.39), channel_id=1, source_target_pairs={{0,16},{8,24},{16,0},{24,8},{1,17},{9,25},{17,1},{25,9},{2,18},{10... | collective-permute-start | bytes 786440 | tf_op jit(solution)/shard_map/ppermute | solution.py:230
  42.1 14.2 %collective-permute-start.3 = (f32[2,2,2,128,128]{4,3,1,2,0:T(8,128)S(1)}, f32[2,2,2,128,128]{4,3,1,2,0:T(8,128)S(1)}, u32[]{:S(2)}, u32[]{:S(2)}) collective-permute-start(f32[2,2,2,128,128]{4,3,1,2,0:T(8,128)S(1)} %pad_maximum_fusion.5), channel_id=1, source_target_pairs={{0,16},{8,24},{16,0},{24,8},{1,17},{9,25},{17,1},{25,9},{2,18},{10... | collective-permute-start | bytes 1572872 | tf_op jit(solution)/shard_map/ppermute | solution.py:230
  46.3 12.2 %collective-permute-start.5 = (f32[2,2,2,128,128]{4,3,1,2,0:T(8,128)S(1)}, f32[2,2,2,128,128]{4,3,1,2,0:T(8,128)S(1)}, u32[]{:S(2)}, u32[]{:S(2)}) collective-permute-start(f32[2,2,2,128,128]{4,3,1,2,0:T(8,128)S(1)} %pad_maximum_fusion.6), channel_id=1, source_target_pairs={{0,8},{8,0},{16,24},{24,16},{1,9},{9,1},{17,25},{25,17},{2,10},{10... | collective-permute-start | bytes 1572872 | tf_op jit(solution)/shard_map/ppermute | solution.py:230
  48.2 21.6 %collective-permute-start.8 = (f32[2,2,2,128,128]{4,3,2,1,0:T(8,128)S(1)}, f32[2,2,2,128,128]{4,3,2,1,0:T(8,128)S(1)}, u32[]{:S(2)}, u32[]{:S(2)}) collective-permute-start(f32[2,2,2,128,128]{4,3,2,1,0:T(8,128)S(1)} %dynamic-slice_bitcast_fusion.1), channel_id=1, source_target_pairs={{0,8},{8,0},{16,24},{24,16},{1,9},{9,1},{17,25},{25,17},{2,10},{10... | collective-permute-start | bytes 1572872 | tf_op jit(solution)/shard_map/ppermute | solution.py:230
  50.7 20.5 %collective-permute-start.18 = (f32[2,2,2,128,128]{4,3,2,1,0:T(8,128)S(1)}, f32[2,2,2,128,128]{4,3,2,1,0:T(8,128)S(1)}, u32[]{:S(2)}, u32[]{:S(2)}) collective-permute-start(f32[2,2,2,128,128]{4,3,2,1,0:T(8,128)S(1)} %dynamic-slice_bitcast_fusion), channel_id=1, source_target_pairs={{0,16},{8,24},{16,0},{24,8},{1,17},{9,25},{17,1},{25,9},{2,18},{10... | collective-permute-start | bytes 1572872 | tf_op jit(solution)/shard_map/ppermute | solution.py:230
  59.0 42.7 %collective-permute-start.6 = (f32[4,4,256,128]{3,2,1,0:T(8,128)S(1)}, f32[4,4,256,128]{3,2,1,0:T(8,128)S(1)}, u32[]{:S(2)}, u32[]{:S(2)}) collective-permute-start(f32[4,4,256,128]{3,2,1,0:T(8,128)S(1)} %pad_maximum_fusion.own_ref), channel_id=1, source_target_pairs={{0,1},{1,0},{2,3},{3,2},{4,5},{5,4},{6,7},{7,6},{8,9},{9,8},{10,11... | collective-permute-start | bytes 6291464 | tf_op jit(solution)/shard_map/ppermute | solution.py:230
  77.1 6.1 %collective-permute-start.20 = (f32[2,128,128]{2,1,0:T(8,128)S(1)}, f32[2,128,128]{2,1,0:T(8,128)S(1)}, u32[]{:S(2)}, u32[]{:S(2)}) collective-permute-start(f32[2,128,128]{2,1,0:T(8,128)S(1)} %dynamic-slice_bitcast_fusion.4), channel_id=1, source_target_pairs={{0,2},{1,3},{2,0},{3,1},{4,6},{5,7},{6,4},{7,5},{8,10},{9,11},{10,... | collective-permute-start | bytes 393224 | tf_op jit(solution)/shard_map/ppermute | solution.py:230
  79.8 6.4 %collective-permute-start.11 = (f32[2,128,128]{2,1,0:T(8,128)S(1)}, f32[2,128,128]{2,1,0:T(8,128)S(1)}, u32[]{:S(2)}, u32[]{:S(2)}) collective-permute-start(f32[2,128,128]{2,1,0:T(8,128)S(1)} %bitcast_add_fusion.5), channel_id=1, source_target_pairs={{0,4},{1,5},{2,6},{3,7},{4,0},{5,1},{6,2},{7,3},{8,12},{9,13},{10,... | collective-permute-start | bytes 393224 | tf_op jit(solution)/shard_map/ppermute | solution.py:230
  83.2 6.6 %collective-permute-start.21 = (f32[2,128,128]{2,1,0:T(8,128)S(1)}, f32[2,128,128]{2,1,0:T(8,128)S(1)}, u32[]{:S(2)}, u32[]{:S(2)}) collective-permute-start(f32[2,128,128]{2,1,0:T(8,128)S(1)} %bitcast_add_fusion.4), channel_id=1, source_target_pairs={{0,4},{1,5},{2,6},{3,7},{4,0},{5,1},{6,2},{7,3},{8,12},{9,13},{10,... | collective-permute-start | bytes 393224 | tf_op jit(solution)/shard_map/ppermute | solution.py:230
  86.2 6.8 %collective-permute-start.12 = (f32[2,128,128]{2,1,0:T(8,128)S(1)}, f32[2,128,128]{2,1,0:T(8,128)S(1)}, u32[]{:S(2)}, u32[]{:S(2)}) collective-permute-start(f32[2,128,128]{2,1,0:T(8,128)S(1)} %add.70), channel_id=1, source_target_pairs={{0,2},{1,3},{2,0},{3,1},{4,6},{5,7},{6,4},{7,5},{8,10},{9,11},{10,... | collective-permute-start | bytes 393224 | tf_op jit(solution)/shard_map/ppermute | solution.py:230
  89.9 9.9 %collective-permute-start.22 = (f32[2,128,128]{2,1,0:T(8,128)S(1)}, f32[2,128,128]{2,1,0:T(8,128)S(1)}, u32[]{:S(2)}, u32[]{:S(2)}) collective-permute-start(f32[2,128,128]{2,1,0:T(8,128)S(1)} %add.75), channel_id=1, source_target_pairs={{0,2},{1,3},{2,0},{3,1},{4,6},{5,7},{6,4},{7,5},{8,10},{9,11},{10,... | collective-permute-start | bytes 393224 | tf_op jit(solution)/shard_map/ppermute | solution.py:230
  93.1 9.6 %collective-permute-start.13 = (f32[128,512]{1,0:T(8,128)S(1)}, f32[128,512]{1,0:T(8,128)S(1)}, u32[]{:S(2)}, u32[]{:S(2)}) collective-permute-start(f32[128,512]{1,0:T(8,128)S(1)} %bitcast.102), channel_id=1, source_target_pairs={{0,1},{1,0},{2,3},{3,2},{4,5},{5,4},{6,7},{7,6},{8,9},{9,8},{10,11... | collective-permute-start | bytes 786440 | tf_op jit(solution)/shard_map/ppermute | solution.py:230
  103.3 7.9 %collective-permute-start.14 = (f32[128,512]{1,0:T(8,128)S(1)}, f32[128,512]{1,0:T(8,128)S(1)}, u32[]{:S(2)}, u32[]{:S(2)}) collective-permute-start(f32[128,512]{1,0:T(8,128)S(1)} %turned.2), channel_id=1, source_target_pairs={{0,16},{8,24},{16,0},{24,8},{1,17},{9,25},{17,1},{25,9},{2,18},{10... | collective-permute-start | bytes 786440 | tf_op jit(solution)/shard_map/ppermute | solution.py:230
  105.4 7.7 %collective-permute-start.24 = (f32[128,512]{1,0:T(8,128)S(1)}, f32[128,512]{1,0:T(8,128)S(1)}, u32[]{:S(2)}, u32[]{:S(2)}) collective-permute-start(f32[128,512]{1,0:T(8,128)S(1)} %turned.3), channel_id=1, source_target_pairs={{0,8},{8,0},{16,24},{24,16},{1,9},{9,1},{17,25},{25,17},{2,10},{10... | collective-permute-start | bytes 786440 | tf_op jit(solution)/shard_map/ppermute | solution.py:230
  111.4 12.7 %collective-permute-start.15 = (f32[2,128,512]{2,1,0:T(8,128)S(1)}, f32[2,128,512]{2,1,0:T(8,128)S(1)}, u32[]{:S(2)}, u32[]{:S(2)}) collective-permute-start(f32[2,128,512]{2,1,0:T(8,128)S(1)} %pad_maximum_fusion.7), channel_id=1, source_target_pairs={{0,8},{8,0},{16,24},{24,16},{1,9},{9,1},{17,25},{25,17},{2,10},{10... | collective-permute-start | bytes 1572872 | tf_op jit(solution)/shard_map/ppermute | solution.py:230
  113.2 12.9 %collective-permute-start.25 = (f32[2,128,512]{2,1,0:T(8,128)S(1)}, f32[2,128,512]{2,1,0:T(8,128)S(1)}, u32[]{:S(2)}, u32[]{:S(2)}) collective-permute-start(f32[2,128,512]{2,1,0:T(8,128)S(1)} %pad_maximum_fusion.8), channel_id=1, source_target_pairs={{0,16},{8,24},{16,0},{24,8},{1,17},{9,25},{17,1},{25,9},{2,18},{10... | collective-permute-start | bytes 1572872 | tf_op jit(solution)/shard_map/ppermute | solution.py:230
  124.3 17.1 %collective-permute-start.16 = (f32[512,512]{1,0:T(8,128)S(1)}, f32[512,512]{1,0:T(8,128)S(1)}, u32[]{:S(2)}, u32[]{:S(2)}) collective-permute-start(f32[512,512]{1,0:T(8,128)S(1)} %bitcast.98), channel_id=1, source_target_pairs={{0,1},{1,0},{2,3},{3,2},{4,5},{5,4},{6,7},{7,6},{8,9},{9,8},{10,11... | collective-permute-start | bytes 3145736 | tf_op jit(solution)/shard_map/ppermute | solution.py:230
  126.3 19.4 %collective-permute-start.26 = (f32[512,512]{1,0:T(8,128)S(1)}, f32[512,512]{1,0:T(8,128)S(1)}, u32[]{:S(2)}, u32[]{:S(2)}) collective-permute-start(f32[512,512]{1,0:T(8,128)S(1)} %bitcast.100), channel_id=1, source_target_pairs={{0,1},{1,0},{2,3},{3,2},{4,5},{5,4},{6,7},{7,6},{8,9},{9,8},{10,11... | collective-permute-start | bytes 3145736 | tf_op jit(solution)/shard_map/ppermute | solution.py:230
  127.9 6.3 %collective-permute-start.27 = (f32[256,128]{1,0:T(8,128)S(1)}, f32[256,128]{1,0:T(8,128)S(1)}, u32[]{:S(2)}, u32[]{:S(2)}) collective-permute-start(f32[256,128]{1,0:T(8,128)S(1)} %pad_maximum_fusion.13), channel_id=1, source_target_pairs={{0,0},{1,4},{2,1},{3,5},{4,2},{5,6},{6,3},{7,7},{8,8},{9,12},{10,9... | collective-permute-start | bytes 393224 | tf_op jit(solution)/shard_map/ppermute | solution.py:304
  (11 other events, 70.4 us)

commit v2 on v1

v2 whole, which is shorter than its diff:
```python
import functools

import jax
import jax.numpy as jnp
from jax import lax
from jax.experimental import pallas as pl
from jax.experimental.pallas import tpu as pltpu
from jax.sharding import PartitionSpec as P


F32, BF16 = jnp.float32, jnp.bfloat16
CHAINS = 2


def split(x):
    high = x.astype(BF16)
    return high, (x - high.astype(F32)).astype(BF16)


def mm(a, b, dims=((1,), (0,))):
    return lax.dot_general(a, b, (dims, ((), ())), preferred_element_type=F32)


def mm3(a, b):
    (ah, al), (bh, bl) = a, b
    return mm(ah, bh) + (mm(al, bh) + mm(ah, bl))


def cost(flops, nbytes):
    return pl.CostEstimate(flops=flops, bytes_accessed=nbytes, transcendentals=0)


def params(mib):
    return pltpu.CompilerParams(dimension_semantics=("arbitrary",), vmem_limit_bytes=mib << 20)


def column(x):
    n, lanes = x.shape
    eye = lax.broadcasted_iota(jnp.int32, (lanes, lanes), 0) == lax.broadcasted_iota(jnp.int32, (lanes, lanes), 1)
    return jnp.concatenate([jnp.sum(jnp.where(eye, x[i : i + 1], 0.0), 1, keepdims=True) for i in range(n)], 0)


def pieces_of(x, out, dims):
    G, Z, b, bc = dims
    for g in range(G):
        for z in range(Z):
            out[g, z] = x[g * b : (g + 1) * b, z * bc : (z + 1) * bc]


def first_kernel(dims, core_ref, psi_ref, vpsi_ref, kin_ref, *rest):
    G, _, b, _ = dims
    outs, (ph_ref, pl_ref, hh_ref, hl_ref, th_ref, tl_ref, acc, right) = rest[:CHAINS], rest[CHAINS:]
    r = pl.program_id(0)
    psi = psi_ref[...]
    h = column(kin_ref[0]) * psi + vpsi_ref[...]
    ph, pl_ = split(psi)
    hh, hl = split(h)
    _, n = psi.shape
    half = n // 2
    hh_ref[...], hl_ref[...] = hh, hl
    rows = [slice((g * CHAINS + k) * b, (g * CHAINS + k + 1) * b) for k in range(CHAINS) for g in range(G)]
    for k in range(CHAINS):
        ph_ref[k] = jnp.concatenate([ph[:, at] for at in rows[k * G : (k + 1) * G]], 1)
        pl_ref[k] = jnp.concatenate([pl_[:, at] for at in rows[k * G : (k + 1) * G]], 1)
    th = jnp.concatenate([ph[:, at] for at in rows], 1).T
    tl = jnp.concatenate([pl_[:, at] for at in rows], 1).T
    th_ref[...], tl_ref[...] = th, tl
    left = jnp.concatenate([th, tl, th], 1)
    right[...] = jnp.concatenate([hh, hh, hl], 0)
    w = 256
    sib = (1 - core_ref[0]) * half

    @pl.when(r == 0)
    def _():
        acc[...] = jnp.zeros_like(acc)

    for j in range(0, half, w):
        acc[:, j : j + w] += mm(left, right[:, pl.ds(pl.multiple_of(sib + j, w), w)])

    @pl.when(r == pl.num_programs(0) - 1)
    def _():
        for k in range(CHAINS):
            pieces_of(acc[k * G * b : (k + 1) * G * b, :], outs[k], dims)


def first(core, psi, vpsi, kin, dims):
    G, _, b, _ = dims
    rows, bands = psi.shape
    t = 256
    blk = pl.BlockSpec((t, bands), lambda i, c: (i, 0))
    piece = pl.BlockSpec(dims, lambda i, c: (0, 0, 0, 0))
    chain = pl.BlockSpec((CHAINS, t, G * b), lambda i, c: (0, i, 0))
    turn = pl.BlockSpec((bands, t), lambda i, c: (0, i))
    return pl.pallas_call(
        functools.partial(first_kernel, dims),
        grid_spec=pltpu.PrefetchScalarGridSpec(
            num_scalar_prefetch=1,
            grid=(rows // t,),
            in_specs=[blk, blk, pl.BlockSpec((1, t // 128, 128), lambda i, c: (i, 0, 0))],
            out_specs=[piece] * CHAINS + [chain] * 2 + [blk] * 2 + [turn] * 2,
            scratch_shapes=[pltpu.VMEM((bands, bands // 2), F32), pltpu.VMEM((3 * t, bands), BF16)],
        ),
        out_shape=[jax.ShapeDtypeStruct(dims, F32)] * CHAINS
        + [pltpu.HBM((CHAINS, rows, G * b), BF16)] * 2
        + [jax.ShapeDtypeStruct((rows, bands), BF16)] * 2
        + [jax.ShapeDtypeStruct((bands, rows), BF16)] * 2,
        compiler_params=params(20),
        cost_estimate=cost(3 * rows * bands * bands, 12 * rows * bands),
        name="first",
    )(core, *(pltpu.with_memory_space_constraint(x, pltpu.HBM) for x in (psi, vpsi)), kin.reshape(rows // t, t // 128, 128))


def second_kernel(dims, core_ref, th_ref, tl_ref, hh_ref, hl_ref, *outs):
    left = jnp.concatenate([th_ref[...], tl_ref[...], th_ref[...]], 1)
    right = jnp.concatenate([hh_ref[...], hh_ref[...], hl_ref[...]], 0)
    pieces_of(mm(left, right), outs[0], dims)


def second(core, turned_psi, h, dims, k):
    G, _, b, _ = dims
    bands, rows = turned_psi[0].shape
    left = pl.BlockSpec((G * b, rows), lambda i, c: (k, 0))
    right = pl.BlockSpec((rows, bands // 2), lambda i, c: (0, c[0]))
    return pl.pallas_call(
        functools.partial(second_kernel, dims),
        grid_spec=pltpu.PrefetchScalarGridSpec(
            num_scalar_prefetch=1,
            grid=(1,),
            in_specs=[left, left, right, right],
            out_specs=pl.BlockSpec(dims, lambda i, c: (0, 0, 0, 0)),
        ),
        out_shape=jax.ShapeDtypeStruct(dims, F32),
        compiler_params=params(6),
        cost_estimate=cost(3 * rows * G * b * bands, 4 * rows * bands),
        name="second",
    )(core, *turned_psi, *h)


def joined_kernel(core_ref, own_ref, sib_ref, high_ref, low_ref):
    G, Z, br, bc = own_ref.shape
    core = core_ref[0]
    for c, ref in ((core, own_ref), (1 - core, sib_ref)):
        for g in range(G):
            for z in range(Z):
                at = slice(g * br, (g + 1) * br), pl.ds(pl.multiple_of((2 * z + c) * bc, bc), bc)
                high_ref[at], low_ref[at] = split(ref[g, z])


def joined(core, own, sib):
    G, _, br, bc = own.shape
    bands = G * br
    if bc % 128:
        return split(ordered(own, sib, core[0] == 1, 2).transpose(0, 3, 1, 2, 4).reshape(bands, bands))
    whole = pl.BlockSpec(own.shape, lambda i, c: (0, 0, 0, 0))
    return pl.pallas_call(
        joined_kernel,
        grid_spec=pltpu.PrefetchScalarGridSpec(
            num_scalar_prefetch=1,
            grid=(1,),
            in_specs=[whole, whole],
            out_specs=[pl.BlockSpec((bands, bands), lambda i, c: (0, 0))] * 2,
        ),
        out_shape=[jax.ShapeDtypeStruct((bands, bands), BF16)] * 2,
        compiler_params=params(6),
        cost_estimate=cost(100 * bands * bands, 12 * bands * bands),
        name="joined",
    )(core, own, sib)


def mixed_kernel(hh_ref, hl_ref, mh_ref, ml_ref, out_ref):
    n = mh_ref.shape[1]
    for j in range(n // 512):
        s = slice(j * 512, (j + 1) * 512)
        out_ref[:, s] = mm3((hh_ref[...], hl_ref[...]), (mh_ref[:, s], ml_ref[:, s]))


def mixed(h, m):
    rows, bands = h[0].shape
    t = 512
    blk = pl.BlockSpec((t, bands), lambda i: (i, 0))
    return pl.pallas_call(
        mixed_kernel,
        grid=(rows // t,),
        in_specs=[blk, blk] + [pl.BlockSpec((bands, bands), lambda i: (0, 0))] * 2,
        out_specs=blk,
        out_shape=jax.ShapeDtypeStruct((rows, bands), F32),
        compiler_params=params(20),
        cost_estimate=cost(6 * rows * bands * bands, 16 * rows * bands),
        name="mixed",
    )(*h, *m)


def turned_kernel(core_ref, own_ref, sib_ref, m1h, m1l, m2h, m2l, out_ref):
    out_ref[...] = mm3(split(own_ref[...]), (m1h[...], m1l[...])) + mm3(split(sib_ref[...]), (m2h[...], m2l[...]))


def turned(core, own, sib, m):
    b, half = own.shape
    row = pl.BlockSpec((b, half), lambda i, c: (0, 0))
    m1 = pl.BlockSpec((half, half), lambda i, c: (c[0], c[0]))
    m2 = pl.BlockSpec((half, half), lambda i, c: (1 - c[0], c[0]))
    return pl.pallas_call(
        turned_kernel,
        grid_spec=pltpu.PrefetchScalarGridSpec(
            num_scalar_prefetch=1, grid=(1,), in_specs=[row, row, m1, m1, m2, m2], out_specs=row
        ),
        out_shape=jax.ShapeDtypeStruct((b, half), F32),
        compiler_params=params(5),
        cost_estimate=cost(12 * b * half * half, 8 * half * half),
        name="turned",
    )(core, own, sib, *m, *m)


def less_kernel(core_ref, acc_ref, ph_ref, pl_ref, *rest):
    ws, (out_ref, right) = rest[:CHAINS], rest[-2:]
    kk = CHAINS * ws[0].shape[0]

    @pl.when(pl.program_id(0) == 0)
    def _():
        high, low = split(jnp.concatenate([w[...] for w in ws], 0))
        right[:kk], right[kk : 2 * kk], right[2 * kk :] = high, high, low

    high, low = [ph_ref[k] for k in range(CHAINS)], [pl_ref[k] for k in range(CHAINS)]
    out_ref[...] = acc_ref[...] - mm(jnp.concatenate(high + low + high, 1), right[...])


def less(core, acc, psi, ws, into=None):
    other = into is not None
    rows, bands = acc.shape
    kk, half = ws[0].shape
    t = 512
    blk = pl.BlockSpec((t, half), lambda i, c: (i, 1 - c[0] if other else c[0]))
    part = pl.BlockSpec((CHAINS, t, kk), lambda i, c: (0, i, 0))
    w = pl.BlockSpec((kk, half), lambda i, c: (0, 0))
    return pl.pallas_call(
        less_kernel,
        grid_spec=pltpu.PrefetchScalarGridSpec(
            num_scalar_prefetch=1,
            grid=(rows // t,),
            in_specs=[blk, part, part] + [w] * CHAINS + [pl.BlockSpec(memory_space=pl.ANY)] * other,
            out_specs=blk,
            scratch_shapes=[pltpu.VMEM((3 * CHAINS * kk, half), BF16)],
        ),
        out_shape=pltpu.HBM((rows, bands), F32),
        input_output_aliases={4 + CHAINS: 0} if other else {},
        compiler_params=params(24),
        cost_estimate=cost(3 * rows * kk * CHAINS * bands, 8 * rows * bands),
        name="less",
    )(core, acc, *psi, *ws, *([into] if other else []))


def halves(x, one, axis):
    low, high = (lax.index_in_dim(x, i, axis, keepdims=False) for i in (0, 1))
    return jnp.where(one, high, low), jnp.where(one, low, high)


def hop(x, axis, mask):
    n = lax.axis_size(axis)
    return lax.ppermute(x, axis, [(i, i ^ mask) for i in range(n)])


def ordered(mine, theirs, one, axis):
    return jnp.stack([jnp.where(one, theirs, mine), jnp.where(one, mine, theirs)], axis)


def reduced(x, place, bits, bit):
    keep, give = halves(x, place[bit], bits.index(bit))
    return keep + hop(give, *bit)


def gather(x, place, bits, order, have=()):
    have = list(have)
    for bit in order:
        a = sum(bits.index(other) < bits.index(bit) for other in have)
        got = hop(x, *bit)
        x = ordered(x, got, place[bit], a)
        have.append(bit)
    return x


def after(x, *others):
    if not others:
        return x
    return lax.optimization_barrier((x, *others))[0]


def axis_bits(axis, low):
    n = lax.axis_size(axis)
    return [(axis, 1 << i) for i in range(low, n.bit_length() - 1)][::-1]


def body(psi, vpsi, kinetic, mixing):
    G, C = lax.axis_size("grow"), lax.axis_size("gcol")
    rows, bands = psi.shape
    Z = C // 2
    br, bc, half = bands // G, bands // C, bands // 2
    b = br // CHAINS
    gb, zb = axis_bits("grow", 0), axis_bits("gcol", 1)
    up = gb[::-1]
    place = {bit: (lax.axis_index(bit[0]) & bit[1]) != 0 for bit in gb + zb}
    core1 = (lax.axis_index("gcol") % 2).reshape(1)
    psi, core1, place = lax.optimization_barrier((psi, core1, place))

    dims = (G, Z, b, bc)
    scale = 1.0 / (rows * G * C)
    *theirs, ph, pl_, hh, hl, th, tl = first(core1, psi, vpsi, kinetic, dims)
    ours = [second(core1, (th, tl), (hh, hl), dims, k) for k in range(CHAINS)]

    sums = []
    for k in range(CHAINS):
        q = ours[k] + hop(theirs[k], "gcol", 1)
        sums.append(q.reshape((2,) * (len(gb) + len(zb)) + (b, bc)))
    left = [gb + zb for _ in range(CHAINS)]
    route = [(up if k % 2 == 0 else gb) + zb[:0:-1] for k in range(CHAINS)]
    for i in range(len(route[0])):
        for k in range(CHAINS):
            bit = route[k][i]
            sums[k] = reduced(sums[k], place, left[k], bit)
            left[k] = [other for other in left[k] if other != bit]
    sums = [(q + hop(q, *zb[0])) * scale for q in sums]

    m = gather(after(mixing, theirs[0]), place, zb, zb)
    ma = gather(m[..., : br // 2, :], place, gb, up).reshape(G, Z, br // 2, bc)
    mb = gather(m[..., br // 2 :, :], place, gb, gb).reshape(G, Z, br // 2, bc)
    m_own = jnp.concatenate([ma, mb], 2)
    m_all = joined(core1, m_own, hop(m_own, "gcol", 1))
    acc = mixed((hh, hl), m_all)

    h_parts, w_own, w_sib = [], [], []
    for k, q in enumerate(sums):
        back = gb if k % 2 == 0 else up
        h_parts.append(halves(q, place[zb[0]], 0)[0])
        row = gather(q, place, zb, zb[1:], zb[:1]).reshape(Z, b, bc).transpose(1, 0, 2).reshape(b, half)
        w = turned(core1, row, hop(row, "gcol", 1), m_all)
        w = gather(w, place, gb, back).reshape(G * b, half)
        w_own.append(w)
        w_sib.append(hop(w, "gcol", 1))

    h = jnp.concatenate(h_parts, 0)
    projected = lax.ppermute(h, "gcol", [(i, (i % 2) * Z + i // 2) for i in range(C)])
    near = less(core1, acc, (ph, pl_), w_own)
    return less(core1, acc, (ph, pl_), w_sib, near), projected


def solution(mesh):
    return jax.shard_map(
        body,
        mesh=mesh,
        in_specs=(
            P(("grow", "gcol"), None),
            P(("grow", "gcol"), None),
            P(("grow", "gcol")),
            P("grow", "gcol"),
        ),
        out_specs=(P(("grow", "gcol"), None), P("grow", "gcol")),
        check_vma=False,
    )
```

time: 152 us -> 146 us (0.961)
  the two profiles are of different devices: /device:TPU:1 before, /device:TPU:8 now
where the time goes in v2:
time: 146 us
  waiting for transfers between devices  76.2 us (52%)
  Pallas kernels  33.6 us (23%)
  starting transfers between devices  31.1 us (21%)
  other arithmetic  2.25 us (2%)
  local copies, waits for them, and re-layouts  1.77 us (1%)
    ppermute x27, waiting for transfers between devices, hop(): return lax.ppermute(x, axis, [(i, i ^ mask) for i in range(n)])  70.3 us
    ppermute x27, starting transfers between devices, hop(): return lax.ppermute(x, axis, [(i, i ^ mask) for i in range(n)])  27.9 us
    pallas_call x2, Pallas kernels, less(): pl.pallas_call(less_kernel, grid_spec=pltpu.PrefetchScalarGridSpec(num_sc...  10.7 us
    pallas_call x1, Pallas kernels, first(): pl.pallas_call(functools.partial(first_kernel, dims), grid_spec=pltpu.Pre...  10.1 us
    pallas_call x1, Pallas kernels, mixed(): pl.pallas_call(mixed_kernel, grid=(rows // t,), in_specs=[blk, blk] + [pl...  6.88 us
    ppermute x1, waiting for transfers between devices, body(): lax.ppermute(h, 'gcol', [(i, i % 2 * Z + i // 2) for i in range(C)])  5.92 us
    pallas_call x2, Pallas kernels, second(): pl.pallas_call(functools.partial(second_kernel, dims), grid_spec=pltpu.Pr...  3.61 us
    ppermute x1, starting transfers between devices, body(): lax.ppermute(h, 'gcol', [(i, i % 2 * Z + i // 2) for i in range(C)])  3.19 us
  transfers between devices with their start and end apart: 28, of which 19 were waited for; matrix products, arithmetic and copies ran while one was open for 2% of the time, Pallas kernels for 12%

profile of v2, /device:TPU:8, one launch (start us, length us, event | category | flops | bytes accessed | tf_op | source)
XLA Modules:
  0.0 146.0 jit_solution(14308953360268259807)
XLA Ops:
  1.3 10.1 %first.1 = (f32[4,4,128,128]{3,2,1,0:T(8,128)S(1)}, f32[4,4,128,128]{3,2,1,0:T(8,128)S(1)}, bf16[2,1024,512]{2,1,0:T(8,128)(2,1)}, bf16[2,1024,512]{2,1,0:T(8,12...) custom-call(s32[1]{0:T(128)} %bitcast.core_ref, ...), custom_call_target="tpu_custom_call" | custom-call | flops 3221225472 | bytes 12582912 | tf_op jit(solution)/shard_map/first/pallas_call | solution.py:94
  11.4 2.6 %collective-permute-start = (f32[256,128]{1,0:T(8,128)S(1)}, f32[256,128]{1,0:T(8,128)S(1)}, u32[]{:S(2)}, u32[]{:S(2)}) collective-permute-start(f32[256,128]{1,0:T(8,128)S(1)} %copy-done.3), channel_id=1, source_target_pairs={{0,4},{1,5},{2,6},{3,7},{4,0},{5,1},{6,2},{7,3},{8,12},{9,13},{10,... | collective-permute-start | bytes 393224 | tf_op jit(solution)/shard_map/ppermute | solution.py:259
  14.0 5.5 %collective-permute-done = f32[256,128]{1,0:T(8,128)S(1)} collective-permute-done((f32[256,128]{1,0:T(8,128)S(1)}, f32[256,128]{1,0:T(8,128)S(1)}, u32[]{:S(2)}, u32[]{:S(2)}) %collective-permute-start) | collective-permute-done | bytes 131104 | tf_op jit(solution)/shard_map/ppermute | solution.py:259
  21.4 6.4 %collective-permute-done.1 = f32[2,256,128]{2,1,0:T(8,128)S(1)} collective-permute-done((f32[2,256,128]{2,1,0:T(8,128)S(1)}, f32[2,256,128]{2,1,0:T(8,128)S(1)}, u32[]{:S(2)}, u32[]{:S(2)}) %collective-permute-start.1) | collective-permute-done | bytes 262176 | tf_op jit(solution)/shard_map/ppermute | solution.py:259
  29.4 1.8 %second.3 = f32[4,4,128,128]{3,2,1,0:T(8,128)S(1)} custom-call(s32[1]{0:T(128)} %bitcast.core_ref, bf16[1024,1024]{1,0:T(8,128)(2,1)S(1)} %get-tuple-element.33.th_ref, bf16[1024,1024]{1,0:T(8,128)(2,1)S(1)} %get-tuple-element.34.tl_ref, bf16[1024,1024]{1,0:T(8,128)(2,1)S(1)} %get-tuple-element.21.hh_ref, bf16[1024,1024]{1,0:T(8,128)(2,1)S(1)} %get-tuple-element.22.hl_ref), custom_call_target="tpu_custom_call" | custom-call | flops 1610612736 | bytes 4194304 | tf_op jit(solution)/shard_map/second/pallas_call | solution.py:124
  31.3 1.8 %second.2 = f32[4,4,128,128]{3,2,1,0:T(8,128)S(1)} custom-call(s32[1]{0:T(128)} %bitcast.core_ref, bf16[1024,1024]{1,0:T(8,128)(2,1)S(1)} %get-tuple-element.33.th_ref, bf16[1024,1024]{1,0:T(8,128)(2,1)S(1)} %get-tuple-element.34.tl_ref, bf16[1024,1024]{1,0:T(8,128)(2,1)S(1)} %get-tuple-element.21.hh_ref, bf16[1024,1024]{1,0:T(8,128)(2,1)S(1)} %get-tuple-element.22.hl_ref), custom_call_target="tpu_custom_call" | custom-call | flops 1610612736 | bytes 4194304 | tf_op jit(solution)/shard_map/second/pallas_call | solution.py:124
  37.0 5.3 %collective-permute-done.4 = f32[2,2,128,128]{3,2,0,1:T(8,128)S(1)} collective-permute-done((f32[2,2,128,128]{3,2,0,1:T(8,128)S(1)}, f32[2,2,128,128]{3,2,0,1:T(8,128)S(1)}, u32[]{:S(2)}, u32[]{:S(2)}) %collective-permute-start.4) | collective-permute-done | bytes 262176 | tf_op jit(solution)/shard_map/ppermute | solution.py:259
  46.7 6.8 %collective-permute-done.3 = f32[2,2,2,128,128]{4,3,1,2,0:T(8,128)S(1)} collective-permute-done((f32[2,2,2,128,128]{4,3,1,2,0:T(8,128)S(1)}, f32[2,2,2,128,128]{4,3,1,2,0:T(8,128)S(1)}, u32[]{:S(2)}, u32[]{:S(2)}) %collective-permute-start.3) | collective-permute-done | bytes 524320 | tf_op jit(solution)/shard_map/ppermute | solution.py:259
  53.5 3.7 %collective-permute-done.5 = f32[2,2,2,128,128]{4,3,1,2,0:T(8,128)S(1)} collective-permute-done((f32[2,2,2,128,128]{4,3,1,2,0:T(8,128)S(1)}, f32[2,2,2,128,128]{4,3,1,2,0:T(8,128)S(1)}, u32[]{:S(2)}, u32[]{:S(2)}) %collective-permute-start.5) | collective-permute-done | bytes 524320 | tf_op jit(solution)/shard_map/ppermute | solution.py:259
  58.1 5.4 %collective-permute-done.8 = f32[2,2,2,128,128]{4,3,1,2,0:T(8,128)S(1)} collective-permute-done((f32[2,2,2,128,128]{4,3,1,2,0:T(8,128)S(1)}, f32[2,2,2,128,128]{4,3,1,2,0:T(8,128)S(1)}, u32[]{:S(2)}, u32[]{:S(2)}) %collective-permute-start.8) | collective-permute-done | bytes 524320 | tf_op jit(solution)/shard_map/ppermute | solution.py:259
  65.9 4.1 %collective-permute-done.9 = f32[2,2,128,128]{3,2,0,1:T(8,128)S(1)} collective-permute-done((f32[2,2,128,128]{3,2,0,1:T(8,128)S(1)}, f32[2,2,128,128]{3,2,0,1:T(8,128)S(1)}, u32[]{:S(2)}, u32[]{:S(2)}) %collective-permute-start.9) | collective-permute-done | bytes 262176 | tf_op jit(solution)/shard_map/ppermute | solution.py:259
  72.3 3.8 %collective-permute-done.10 = f32[2,128,128]{2,1,0:T(8,128)S(1)} collective-permute-done((f32[2,128,128]{2,1,0:T(8,128)S(1)}, f32[2,128,128]{2,1,0:T(8,128)S(1)}, u32[]{:S(2)}, u32[]{:S(2)}) %collective-permute-start.10) | collective-permute-done | bytes 131104 | tf_op jit(solution)/shard_map/ppermute | solution.py:259
  76.1 3.9 %collective-permute-start.11 = (f32[2,128,128]{2,1,0:T(8,128)S(1)}, f32[2,128,128]{2,1,0:T(8,128)S(1)}, u32[]{:S(2)}, u32[]{:S(2)}) collective-permute-start(f32[2,128,128]{2,1,0:T(8,128)S(1)} %bitcast_add_fusion.4), channel_id=1, source_target_pairs={{0,4},{1,5},{2,6},{3,7},{4,0},{5,1},{6,2},{7,3},{8,12},{9,13},{10,... | collective-permute-start | bytes 393224 | tf_op jit(solution)/shard_map/ppermute | solution.py:259
  80.0 2.8 %collective-permute-start.21 = (f32[2,128,128]{2,1,0:T(8,128)S(1)}, f32[2,128,128]{2,1,0:T(8,128)S(1)}, u32[]{:S(2)}, u32[]{:S(2)}) collective-permute-start(f32[2,128,128]{2,1,0:T(8,128)S(1)} %bitcast_add_fusion.3), channel_id=1, source_target_pairs={{0,4},{1,5},{2,6},{3,7},{4,0},{5,1},{6,2},{7,3},{8,12},{9,13},{10,... | collective-permute-start | bytes 393224 | tf_op jit(solution)/shard_map/ppermute | solution.py:259
  82.8 2.4 %collective-permute-done.11 = f32[2,128,128]{2,1,0:T(8,128)S(1)} collective-permute-done((f32[2,128,128]{2,1,0:T(8,128)S(1)}, f32[2,128,128]{2,1,0:T(8,128)S(1)}, u32[]{:S(2)}, u32[]{:S(2)}) %collective-permute-start.11) | collective-permute-done | bytes 131104 | tf_op jit(solution)/shard_map/ppermute | solution.py:259
  87.9 2.4 %collective-permute-done.12 = f32[2,128,128]{2,1,0:T(8,128)S(1)} collective-permute-done((f32[2,128,128]{2,1,0:T(8,128)S(1)}, f32[2,128,128]{2,1,0:T(8,128)S(1)}, u32[]{:S(2)}, u32[]{:S(2)}) %collective-permute-start.12) | collective-permute-done | bytes 131104 | tf_op jit(solution)/shard_map/ppermute | solution.py:259
  93.6 1.6 %collective-permute-start.14 = (f32[128,512]{1,0:T(8,128)S(1)}, f32[128,512]{1,0:T(8,128)S(1)}, u32[]{:S(2)}, u32[]{:S(2)}) collective-permute-start(f32[128,512]{1,0:T(8,128)S(1)} %turned.2), channel_id=1, source_target_pairs={{0,16},{8,24},{16,0},{24,8},{1,17},{9,25},{17,1},{25,9},{2,18},{10... | collective-permute-start | bytes 786440 | tf_op jit(solution)/shard_map/ppermute | solution.py:259
  96.4 6.0 %collective-permute-done.14 = f32[128,512]{1,0:T(8,128)S(1)} collective-permute-done((f32[128,512]{1,0:T(8,128)S(1)}, f32[128,512]{1,0:T(8,128)S(1)}, u32[]{:S(2)}, u32[]{:S(2)}) %collective-permute-start.14) | collective-permute-done | bytes 262176 | tf_op jit(solution)/shard_map/ppermute | solution.py:259
  105.0 11.0 %collective-permute-done.15 = f32[2,128,512]{2,1,0:T(8,128)S(1)} collective-permute-done((f32[2,128,512]{2,1,0:T(8,128)S(1)}, f32[2,128,512]{2,1,0:T(8,128)S(1)}, u32[]{:S(2)}, u32[]{:S(2)}) %collective-permute-start.15) | collective-permute-done | bytes 524320 | tf_op jit(solution)/shard_map/ppermute | solution.py:259
  118.5 3.2 %collective-permute-start.27 = (f32[256,128]{1,0:T(8,128)S(1)}, f32[256,128]{1,0:T(8,128)S(1)}, u32[]{:S(2)}, u32[]{:S(2)}) collective-permute-start(f32[256,128]{1,0:T(8,128)S(1)} %pad_maximum_fusion.13), channel_id=1, source_target_pairs={{0,0},{1,4},{2,1},{3,5},{4,2},{5,6},{6,3},{7,7},{8,8},{9,12},{10,9... | collective-permute-start | bytes 393224 | tf_op jit(solution)/shard_map/ppermute | solution.py:340
  121.7 5.9 %collective-permute-done.27 = f32[256,128]{1,0:T(8,128)S(1)} collective-permute-done((f32[256,128]{1,0:T(8,128)S(1)}, f32[256,128]{1,0:T(8,128)S(1)}, u32[]{:S(2)}, u32[]{:S(2)}) %collective-permute-start.27) | collective-permute-done | bytes 131104 | tf_op jit(solution)/shard_map/ppermute | solution.py:340
  127.7 6.9 %mixed.1.acc_ref = f32[1024,1024]{1,0:T(8,128)S(1)} custom-call(bf16[1024,1024]{1,0:T(8,128)(2,1)S(1)} %get-tuple-element.21.hh_ref, bf16[1024,1024]{1,0:T(8,128)(2,1)S(1)} %get-tuple-element.22.hl_ref, bf16[1024,1024]{1,0:T(8,128)(2,1)S(1)} %get-tuple-element.29.mh_ref.m1h.m2h, bf16[1024,1024]{1,0:T(8,128)(2,1)S(1)} %get-tuple-element.30.ml_ref.m1l.m2l), custom_call_target="tpu_custom_call" | custom-call | flops 6442450944 | bytes 16777216 | tf_op jit(solution)/shard_map/mixed/pallas_call | solution.py:181
  134.6 5.4 %less.2.rest_2_ = f32[1024,1024]{1,0:T(8,128)} custom-call(s32[1]{0:T(128)} %bitcast.core_ref, f32[1024,1024]{1,0:T(8,128)S(1)} %mixed.1.acc_ref, bf16[2,1024,512]{2,1,0:T(8,128)(2,1)S(1)} %copy-done, bf16[2,1024,512]{2,1,0:T(8,128)(2,1)S(1)} %copy-done.1, f32[512,512]{1,0:T(8,128)S(1)} %bitcast.98, f32[512,512]{1,0:T(8,128)S(1)} %bitcast.100), custom_call_target="tpu_custom_call" | custom-call | flops 3221225472 | bytes 8388608 | tf_op jit(solution)/shard_map/less/pallas_call | solution.py:235
  139.9 5.4 %less.3 = f32[1024,1024]{1,0:T(8,128)} custom-call(s32[1]{0:T(128)} %bitcast.core_ref, f32[1024,1024]{1,0:T(8,128)S(1)} %mixed.1.acc_ref, bf16[2,1024,512]{2,1,0:T(8,128)(2,1)S(1)} %copy-done, bf16[2,1024,512]{2,1,0:T(8,128)(2,1)S(1)} %copy-done.1, f32[512,512]{1,0:T(8,128)S(1)} %collective-permute-done.16.rest_0_, ...), custom_call_target="tpu_custom_call", output_to_operand_aliasing={{}: (6, {})} | custom-call | flops 3221225472 | bytes 8388608 | tf_op jit(solution)/shard_map/less/pallas_call | solution.py:235
  (101 shorter events, 30.7 us)
Async XLA Ops:
  11.4 8.0 %collective-permute-start = (f32[256,128]{1,0:T(8,128)S(1)}, f32[256,128]{1,0:T(8,128)S(1)}, u32[]{:S(2)}, u32[]{:S(2)}) collective-permute-start(f32[256,128]{1,0:T(8,128)S(1)} %copy-done.3), channel_id=1, source_target_pairs={{0,4},{1,5},{2,6},{3,7},{4,0},{5,1},{6,2},{7,3},{8,12},{9,13},{10,... | collective-permute-start | bytes 393224 | tf_op jit(solution)/shard_map/ppermute | solution.py:259
  19.5 8.3 %collective-permute-start.1 = (f32[2,256,128]{2,1,0:T(8,128)S(1)}, f32[2,256,128]{2,1,0:T(8,128)S(1)}, u32[]{:S(2)}, u32[]{:S(2)}) collective-permute-start(f32[2,256,128]{2,1,0:T(8,128)S(1)} %pad_maximum_fusion.10), channel_id=1, source_target_pairs={{0,2},{1,3},{2,0},{3,1},{4,6},{5,7},{6,4},{7,5},{8,10},{9,11},{10,... | collective-permute-start | bytes 786440 | tf_op jit(solution)/shard_map/ppermute | solution.py:259
  20.9 24.0 %collective-permute-start.7 = (f32[4,4,128,128]{3,2,1,0:T(8,128)S(1)}, f32[4,4,128,128]{3,2,1,0:T(8,128)S(1)}, u32[]{:S(2)}, u32[]{:S(2)}) collective-permute-start(f32[4,4,128,128]{3,2,1,0:T(8,128)S(1)} %get-tuple-element.27), channel_id=1, source_target_pairs={{0,1},{1,0},{2,3},{3,2},{4,5},{5,4},{6,7},{7,6},{8,9},{9,8},{10,11... | collective-permute-start | bytes 3145736 | tf_op jit(solution)/shard_map/ppermute | solution.py:259
  20.9 22.1 %collective-permute-start.17 = (f32[4,4,128,128]{3,2,1,0:T(8,128)S(1)}, f32[4,4,128,128]{3,2,1,0:T(8,128)S(1)}, u32[]{:S(2)}, u32[]{:S(2)}) collective-permute-start(f32[4,4,128,128]{3,2,1,0:T(8,128)S(1)} %get-tuple-element.35), channel_id=1, source_target_pairs={{0,1},{1,0},{2,3},{3,2},{4,5},{5,4},{6,7},{7,6},{8,9},{9,8},{10,11... | collective-permute-start | bytes 3145736 | tf_op jit(solution)/shard_map/ppermute | solution.py:259
  27.9 7.4 %collective-permute-start.2 = (f32[2,2,128,128]{3,2,0,1:T(8,128)S(1)}, f32[2,2,128,128]{3,2,0,1:T(8,128)S(1)}, u32[]{:S(2)}, u32[]{:S(2)}) collective-permute-start(f32[2,2,128,128]{3,2,0,1:T(8,128)S(1)} %get-tuple-element.54), channel_id=1, source_target_pairs={{0,8},{8,0},{16,24},{24,16},{1,9},{9,1},{17,25},{25,17},{2,10},{10... | collective-permute-start | bytes 786440 | tf_op jit(solution)/shard_map/ppermute | solution.py:259
  33.1 9.2 %collective-permute-start.4 = (f32[2,2,128,128]{3,2,0,1:T(8,128)S(1)}, f32[2,2,128,128]{3,2,0,1:T(8,128)S(1)}, u32[]{:S(2)}, u32[]{:S(2)}) collective-permute-start(f32[2,2,128,128]{3,2,0,1:T(8,128)S(1)} %get-tuple-element.55), channel_id=1, source_target_pairs={{0,16},{8,24},{16,0},{24,8},{1,17},{9,25},{17,1},{25,9},{2,18},{10... | collective-permute-start | bytes 786440 | tf_op jit(solution)/shard_map/ppermute | solution.py:259
  35.4 18.1 %collective-permute-start.3 = (f32[2,2,2,128,128]{4,3,1,2,0:T(8,128)S(1)}, f32[2,2,2,128,128]{4,3,1,2,0:T(8,128)S(1)}, u32[]{:S(2)}, u32[]{:S(2)}) collective-permute-start(f32[2,2,2,128,128]{4,3,1,2,0:T(8,128)S(1)} %pad_maximum_fusion.5), channel_id=1, source_target_pairs={{0,16},{8,24},{16,0},{24,8},{1,17},{9,25},{17,1},{25,9},{2,18},{10... | collective-permute-start | bytes 1572872 | tf_op jit(solution)/shard_map/ppermute | solution.py:259
  42.4 14.9 %collective-permute-start.5 = (f32[2,2,2,128,128]{4,3,1,2,0:T(8,128)S(1)}, f32[2,2,2,128,128]{4,3,1,2,0:T(8,128)S(1)}, u32[]{:S(2)}, u32[]{:S(2)}) collective-permute-start(f32[2,2,2,128,128]{4,3,1,2,0:T(8,128)S(1)} %pad_maximum_fusion.6), channel_id=1, source_target_pairs={{0,8},{8,0},{16,24},{24,16},{1,9},{9,1},{17,25},{25,17},{2,10},{10... | collective-permute-start | bytes 1572872 | tf_op jit(solution)/shard_map/ppermute | solution.py:259
  43.3 21.9 %collective-permute-start.18 = (f32[2,2,2,128,128]{4,3,1,2,0:T(8,128)S(1)}, f32[2,2,2,128,128]{4,3,1,2,0:T(8,128)S(1)}, u32[]{:S(2)}, u32[]{:S(2)}) collective-permute-start(f32[2,2,2,128,128]{4,3,1,2,0:T(8,128)S(1)} %copy.21), channel_id=1, source_target_pairs={{0,16},{8,24},{16,0},{24,8},{1,17},{9,25},{17,1},{25,9},{2,18},{10... | collective-permute-start | bytes 1572872 | tf_op jit(solution)/shard_map/ppermute | solution.py:259
  45.2 18.3 %collective-permute-start.8 = (f32[2,2,2,128,128]{4,3,1,2,0:T(8,128)S(1)}, f32[2,2,2,128,128]{4,3,1,2,0:T(8,128)S(1)}, u32[]{:S(2)}, u32[]{:S(2)}) collective-permute-start(f32[2,2,2,128,128]{4,3,1,2,0:T(8,128)S(1)} %select_bitcast_fusion.4), channel_id=1, source_target_pairs={{0,8},{8,0},{16,24},{24,16},{1,9},{9,1},{17,25},{25,17},{2,10},{10... | collective-permute-start | bytes 1572872 | tf_op jit(solution)/shard_map/ppermute | solution.py:259
  58.0 33.9 %collective-permute-start.6 = (f32[4,4,256,128]{3,2,1,0:T(8,128)S(1)}, f32[4,4,256,128]{3,2,1,0:T(8,128)S(1)}, u32[]{:S(2)}, u32[]{:S(2)}) collective-permute-start(f32[4,4,256,128]{3,2,1,0:T(8,128)S(1)} %pad_maximum_fusion.own_ref), channel_id=1, source_target_pairs={{0,1},{1,0},{2,3},{3,2},{4,5},{5,4},{6,7},{7,6},{8,9},{9,8},{10,11... | collective-permute-start | bytes 6291464 | tf_op jit(solution)/shard_map/ppermute | solution.py:259
  63.6 6.4 %collective-permute-start.9 = (f32[2,2,128,128]{3,2,0,1:T(8,128)S(1)}, f32[2,2,128,128]{3,2,0,1:T(8,128)S(1)}, u32[]{:S(2)}, u32[]{:S(2)}) collective-permute-start(f32[2,2,128,128]{3,2,0,1:T(8,128)S(1)} %select_bitcast_fusion.14), channel_id=1, source_target_pairs={{0,16},{8,24},{16,0},{24,8},{1,17},{9,25},{17,1},{25,9},{2,18},{10... | collective-permute-start | bytes 786440 | tf_op jit(solution)/shard_map/ppermute | solution.py:259
  65.3 6.4 %collective-permute-start.19 = (f32[2,2,128,128]{3,2,0,1:T(8,128)S(1)}, f32[2,2,128,128]{3,2,0,1:T(8,128)S(1)}, u32[]{:S(2)}, u32[]{:S(2)}) collective-permute-start(f32[2,2,128,128]{3,2,0,1:T(8,128)S(1)} %select_bitcast_fusion.11), channel_id=1, source_target_pairs={{0,8},{8,0},{16,24},{24,16},{1,9},{9,1},{17,25},{25,17},{2,10},{10... | collective-permute-start | bytes 786440 | tf_op jit(solution)/shard_map/ppermute | solution.py:259
  70.1 6.0 %collective-permute-start.10 = (f32[2,128,128]{2,1,0:T(8,128)S(1)}, f32[2,128,128]{2,1,0:T(8,128)S(1)}, u32[]{:S(2)}, u32[]{:S(2)}) collective-permute-start(f32[2,128,128]{2,1,0:T(8,128)S(1)} %select_bitcast_fusion.26), channel_id=1, source_target_pairs={{0,2},{1,3},{2,0},{3,1},{4,6},{5,7},{6,4},{7,5},{8,10},{9,11},{10,... | collective-permute-start | bytes 393224 | tf_op jit(solution)/shard_map/ppermute | solution.py:259
  71.8 8.2 %collective-permute-start.20 = (f32[2,128,128]{2,1,0:T(8,128)S(1)}, f32[2,128,128]{2,1,0:T(8,128)S(1)}, u32[]{:S(2)}, u32[]{:S(2)}) collective-permute-start(f32[2,128,128]{2,1,0:T(8,128)S(1)} %select_bitcast_fusion.23), channel_id=1, source_target_pairs={{0,2},{1,3},{2,0},{3,1},{4,6},{5,7},{6,4},{7,5},{8,10},{9,11},{10,... | collective-permute-start | bytes 393224 | tf_op jit(solution)/shard_map/ppermute | solution.py:259
  76.1 9.2 %collective-permute-start.11 = (f32[2,128,128]{2,1,0:T(8,128)S(1)}, f32[2,128,128]{2,1,0:T(8,128)S(1)}, u32[]{:S(2)}, u32[]{:S(2)}) collective-permute-start(f32[2,128,128]{2,1,0:T(8,128)S(1)} %bitcast_add_fusion.4), channel_id=1, source_target_pairs={{0,4},{1,5},{2,6},{3,7},{4,0},{5,1},{6,2},{7,3},{8,12},{9,13},{10,... | collective-permute-start | bytes 393224 | tf_op jit(solution)/shard_map/ppermute | solution.py:259
  80.0 6.6 %collective-permute-start.21 = (f32[2,128,128]{2,1,0:T(8,128)S(1)}, f32[2,128,128]{2,1,0:T(8,128)S(1)}, u32[]{:S(2)}, u32[]{:S(2)}) collective-permute-start(f32[2,128,128]{2,1,0:T(8,128)S(1)} %bitcast_add_fusion.3), channel_id=1, source_target_pairs={{0,4},{1,5},{2,6},{3,7},{4,0},{5,1},{6,2},{7,3},{8,12},{9,13},{10,... | collective-permute-start | bytes 393224 | tf_op jit(solution)/shard_map/ppermute | solution.py:259
  93.6 8.8 %collective-permute-start.14 = (f32[128,512]{1,0:T(8,128)S(1)}, f32[128,512]{1,0:T(8,128)S(1)}, u32[]{:S(2)}, u32[]{:S(2)}) collective-permute-start(f32[128,512]{1,0:T(8,128)S(1)} %turned.2), channel_id=1, source_target_pairs={{0,16},{8,24},{16,0},{24,8},{1,17},{9,25},{17,1},{25,9},{2,18},{10... | collective-permute-start | bytes 786440 | tf_op jit(solution)/shard_map/ppermute | solution.py:259
  95.8 8.5 %collective-permute-start.24 = (f32[128,512]{1,0:T(8,128)S(1)}, f32[128,512]{1,0:T(8,128)S(1)}, u32[]{:S(2)}, u32[]{:S(2)}) collective-permute-start(f32[128,512]{1,0:T(8,128)S(1)} %turned.3), channel_id=1, source_target_pairs={{0,8},{8,0},{16,24},{24,16},{1,9},{9,1},{17,25},{25,17},{2,10},{10... | collective-permute-start | bytes 786440 | tf_op jit(solution)/shard_map/ppermute | solution.py:259
  102.5 13.5 %collective-permute-start.15 = (f32[2,128,512]{2,1,0:T(8,128)S(1)}, f32[2,128,512]{2,1,0:T(8,128)S(1)}, u32[]{:S(2)}, u32[]{:S(2)}) collective-permute-start(f32[2,128,512]{2,1,0:T(8,128)S(1)} %pad_maximum_fusion.7), channel_id=1, source_target_pairs={{0,8},{8,0},{16,24},{24,16},{1,9},{9,1},{17,25},{25,17},{2,10},{10... | collective-permute-start | bytes 1572872 | tf_op jit(solution)/shard_map/ppermute | solution.py:259
  104.5 13.3 %collective-permute-start.25 = (f32[2,128,512]{2,1,0:T(8,128)S(1)}, f32[2,128,512]{2,1,0:T(8,128)S(1)}, u32[]{:S(2)}, u32[]{:S(2)}) collective-permute-start(f32[2,128,512]{2,1,0:T(8,128)S(1)} %pad_maximum_fusion.8), channel_id=1, source_target_pairs={{0,16},{8,24},{16,0},{24,8},{1,17},{9,25},{17,1},{25,9},{2,18},{10... | collective-permute-start | bytes 1572872 | tf_op jit(solution)/shard_map/ppermute | solution.py:259
  117.9 22.0 %collective-permute-start.26 = (f32[512,512]{1,0:T(8,128)S(1)}, f32[512,512]{1,0:T(8,128)S(1)}, u32[]{:S(2)}, u32[]{:S(2)}) collective-permute-start(f32[512,512]{1,0:T(8,128)S(1)} %bitcast.99), channel_id=1, source_target_pairs={{0,1},{1,0},{2,3},{3,2},{4,5},{5,4},{6,7},{7,6},{8,9},{9,8},{10,11... | collective-permute-start | bytes 3145736 | tf_op jit(solution)/shard_map/ppermute | solution.py:259
  118.0 21.9 %collective-permute-start.16 = (f32[512,512]{1,0:T(8,128)S(1)}, f32[512,512]{1,0:T(8,128)S(1)}, u32[]{:S(2)}, u32[]{:S(2)}) collective-permute-start(f32[512,512]{1,0:T(8,128)S(1)} %bitcast.97), channel_id=1, source_target_pairs={{0,1},{1,0},{2,3},{3,2},{4,5},{5,4},{6,7},{7,6},{8,9},{9,8},{10,11... | collective-permute-start | bytes 3145736 | tf_op jit(solution)/shard_map/ppermute | solution.py:259
  118.5 9.1 %collective-permute-start.27 = (f32[256,128]{1,0:T(8,128)S(1)}, f32[256,128]{1,0:T(8,128)S(1)}, u32[]{:S(2)}, u32[]{:S(2)}) collective-permute-start(f32[256,128]{1,0:T(8,128)S(1)} %pad_maximum_fusion.13), channel_id=1, source_target_pairs={{0,0},{1,4},{2,1},{3,5},{4,2},{5,6},{6,3},{7,7},{8,8},{9,12},{10,9... | collective-permute-start | bytes 393224 | tf_op jit(solution)/shard_map/ppermute | solution.py:340
  (8 other events, 59.0 us)

commit v3 on v2

--- a/solution.py
+++ b/solution.py
@@ -47,7 +47,7 @@
             out[g, z] = x[g * b : (g + 1) * b, z * bc : (z + 1) * bc]
 
 
-def first_kernel(dims, core_ref, psi_ref, vpsi_ref, kin_ref, *rest):
+def first_kernel(dims, masks, core_ref, psi_ref, vpsi_ref, kin_ref, *rest):
     G, _, b, _ = dims
     outs, (ph_ref, pl_ref, hh_ref, hl_ref, th_ref, tl_ref, acc, right) = rest[:CHAINS], rest[CHAINS:]
     r = pl.program_id(0)
@@ -60,8 +60,10 @@
     hh_ref[...], hl_ref[...] = hh, hl
     rows = [slice((g * CHAINS + k) * b, (g * CHAINS + k + 1) * b) for k in range(CHAINS) for g in range(G)]
     for k in range(CHAINS):
-        ph_ref[k] = jnp.concatenate([ph[:, at] for at in rows[k * G : (k + 1) * G]], 1)
-        pl_ref[k] = jnp.concatenate([pl_[:, at] for at in rows[k * G : (k + 1) * G]], 1)
+        for v in range(2):
+            some = [rows[k * G + g] for g in range(G) if (g & masks[k] != 0) == v]
+            ph_ref[k, v] = jnp.concatenate([ph[:, at] for at in some], 1)
+            pl_ref[k, v] = jnp.concatenate([pl_[:, at] for at in some], 1)
     th = jnp.concatenate([ph[:, at] for at in rows], 1).T
     tl = jnp.concatenate([pl_[:, at] for at in rows], 1).T
     th_ref[...], tl_ref[...] = th, tl
@@ -83,16 +85,16 @@
             pieces_of(acc[k * G * b : (k + 1) * G * b, :], outs[k], dims)
 
 
-def first(core, psi, vpsi, kin, dims):
+def first(core, psi, vpsi, kin, dims, masks):
     G, _, b, _ = dims
     rows, bands = psi.shape
     t = 256
     blk = pl.BlockSpec((t, bands), lambda i, c: (i, 0))
     piece = pl.BlockSpec(dims, lambda i, c: (0, 0, 0, 0))
-    chain = pl.BlockSpec((CHAINS, t, G * b), lambda i, c: (0, i, 0))
+    chain = pl.BlockSpec((CHAINS, 2, t, G * b // 2), lambda i, c: (0, 0, i, 0))
     turn = pl.BlockSpec((bands, t), lambda i, c: (0, i))
     return pl.pallas_call(
-        functools.partial(first_kernel, dims),
+        functools.partial(first_kernel, dims, masks),
         grid_spec=pltpu.PrefetchScalarGridSpec(
             num_scalar_prefetch=1,
             grid=(rows // t,),
@@ -101,7 +103,7 @@
             scratch_shapes=[pltpu.VMEM((bands, bands // 2), F32), pltpu.VMEM((3 * t, bands), BF16)],
         ),
         out_shape=[jax.ShapeDtypeStruct(dims, F32)] * CHAINS
-        + [pltpu.HBM((CHAINS, rows, G * b), BF16)] * 2
+        + [pltpu.HBM((CHAINS, 2, rows, G * b // 2), BF16)] * 2
         + [jax.ShapeDtypeStruct((rows, bands), BF16)] * 2
         + [jax.ShapeDtypeStruct((bands, rows), BF16)] * 2,
         compiler_params=params(20),
@@ -136,35 +138,39 @@
     )(core, *turned_psi, *h)
 
 
-def joined_kernel(core_ref, own_ref, sib_ref, high_ref, low_ref):
-    G, Z, br, bc = own_ref.shape
+def joined_kernel(core_ref, *rest):
+    refs, (high_ref, low_ref) = rest[:4], rest[4:]
+    G, Z, n, bc = refs[0].shape
     core = core_ref[0]
-    for c, ref in ((core, own_ref), (1 - core, sib_ref)):
+    for i, ref in enumerate(refs):
+        c, part = (core if i < 2 else 1 - core), i % 2
         for g in range(G):
+            rows = slice((2 * g + part) * n, (2 * g + part + 1) * n)
             for z in range(Z):
-                at = slice(g * br, (g + 1) * br), pl.ds(pl.multiple_of((2 * z + c) * bc, bc), bc)
+                at = rows, pl.ds(pl.multiple_of((2 * z + c) * bc, bc), bc)
                 high_ref[at], low_ref[at] = split(ref[g, z])
 
 
 def joined(core, own, sib):
-    G, _, br, bc = own.shape
-    bands = G * br
+    G, Z, n, bc = own[0].shape
+    bands = 2 * G * n
     if bc % 128:
+        own, sib = (jnp.stack(x, 2).reshape(G, Z, 2 * n, bc) for x in (own, sib))
         return split(ordered(own, sib, core[0] == 1, 2).transpose(0, 3, 1, 2, 4).reshape(bands, bands))
-    whole = pl.BlockSpec(own.shape, lambda i, c: (0, 0, 0, 0))
+    whole = pl.BlockSpec(own[0].shape, lambda i, c: (0, 0, 0, 0))
     return pl.pallas_call(
         joined_kernel,
         grid_spec=pltpu.PrefetchScalarGridSpec(
             num_scalar_prefetch=1,
             grid=(1,),
-            in_specs=[whole, whole],
+            in_specs=[whole] * 4,
             out_specs=[pl.BlockSpec((bands, bands), lambda i, c: (0, 0))] * 2,
         ),
         out_shape=[jax.ShapeDtypeStruct((bands, bands), BF16)] * 2,
         compiler_params=params(6),
         cost_estimate=cost(100 * bands * bands, 12 * bands * bands),
         name="joined",
-    )(core, own, sib)
+    )(core, *own, *sib)
 
 
 def mixed_kernel(hh_ref, hl_ref, mh_ref, ml_ref, out_ref):
@@ -211,42 +217,49 @@
     )(core, own, sib, *m, *m)
 
 
-def less_kernel(core_ref, acc_ref, ph_ref, pl_ref, *rest):
-    ws, (out_ref, right) = rest[:CHAINS], rest[-2:]
+def less_kernel(at_ref, acc_ref, *rest):
+    high, low = [[x[...] for x in rest[k * CHAINS : (k + 1) * CHAINS]] for k in range(2)]
+    ws, (out_ref, right) = rest[2 * CHAINS : 3 * CHAINS], rest[-2:]
     kk = CHAINS * ws[0].shape[0]
 
     @pl.when(pl.program_id(0) == 0)
     def _():
-        high, low = split(jnp.concatenate([w[...] for w in ws], 0))
-        right[:kk], right[kk : 2 * kk], right[2 * kk :] = high, high, low
-
-    high, low = [ph_ref[k] for k in range(CHAINS)], [pl_ref[k] for k in range(CHAINS)]
+        wh, wl = split(jnp.concatenate([w[...] for w in ws], 0))
+        right[:kk], right[kk : 2 * kk], right[2 * kk :] = wh, wh, wl
+
     out_ref[...] = acc_ref[...] - mm(jnp.concatenate(high + low + high, 1), right[...])
 
 
-def less(core, acc, psi, ws, into=None):
-    other = into is not None
+def less(at, acc, psi, ws, other_core, other_bands, into=None, last=False):
     rows, bands = acc.shape
     kk, half = ws[0].shape
     t = 512
-    blk = pl.BlockSpec((t, half), lambda i, c: (i, 1 - c[0] if other else c[0]))
-    part = pl.BlockSpec((CHAINS, t, kk), lambda i, c: (0, i, 0))
+    more = into is not None
+    blk = pl.BlockSpec((t, half), lambda i, c: (i, 1 - c[0] if other_core else c[0]))
+
+    def part(k):
+        return pl.BlockSpec((None, None, t, kk), lambda i, c: (k, 1 - c[1 + k] if other_bands else c[1 + k], i, 0))
+
     w = pl.BlockSpec((kk, half), lambda i, c: (0, 0))
+    shape = pltpu.HBM((rows, bands), F32) if last else jax.ShapeDtypeStruct((rows, bands), F32)
     return pl.pallas_call(
         less_kernel,
         grid_spec=pltpu.PrefetchScalarGridSpec(
             num_scalar_prefetch=1,
             grid=(rows // t,),
-            in_specs=[blk, part, part] + [w] * CHAINS + [pl.BlockSpec(memory_space=pl.ANY)] * other,
+            in_specs=[blk]
+            + [part(k) for k in range(CHAINS)] * 2
+            + [w] * CHAINS
+            + [pl.BlockSpec(memory_space=pl.ANY)] * more,
             out_specs=blk,
             scratch_shapes=[pltpu.VMEM((3 * CHAINS * kk, half), BF16)],
         ),
-        out_shape=pltpu.HBM((rows, bands), F32),
-        input_output_aliases={4 + CHAINS: 0} if other else {},
-        compiler_params=params(24),
+        out_shape=shape,
+        input_output_aliases={2 + 3 * CHAINS: 0} if more else {},
+        compiler_params=params(20),
         cost_estimate=cost(3 * rows * kk * CHAINS * bands, 8 * rows * bands),
         name="less",
-    )(core, acc, *psi, *ws, *([into] if other else []))
+    )(at, acc, *[x for x in psi for _ in range(CHAINS)], *ws, *([into] if more else []))
 
 
 def halves(x, one, axis):
@@ -299,11 +312,13 @@
     up = gb[::-1]
     place = {bit: (lax.axis_index(bit[0]) & bit[1]) != 0 for bit in gb + zb}
     core1 = (lax.axis_index("gcol") % 2).reshape(1)
-    psi, core1, place = lax.optimization_barrier((psi, core1, place))
+    backs = [gb if k % 2 == 0 else up for k in range(CHAINS)]
+    at = jnp.concatenate([core1] + [place[back[-1]].astype(jnp.int32).reshape(1) for back in backs])
+    psi, core1, at, place = lax.optimization_barrier((psi, core1, at, place))
 
     dims = (G, Z, b, bc)
     scale = 1.0 / (rows * G * C)
-    *theirs, ph, pl_, hh, hl, th, tl = first(core1, psi, vpsi, kinetic, dims)
+    *theirs, ph, pl_, hh, hl, th, tl = first(core1, psi, vpsi, kinetic, dims, [back[-1][1] for back in backs])
     ours = [second(core1, (th, tl), (hh, hl), dims, k) for k in range(CHAINS)]
 
     sums = []
@@ -322,24 +337,30 @@
     m = gather(after(mixing, theirs[0]), place, zb, zb)
     ma = gather(m[..., : br // 2, :], place, gb, up).reshape(G, Z, br // 2, bc)
     mb = gather(m[..., br // 2 :, :], place, gb, gb).reshape(G, Z, br // 2, bc)
-    m_own = jnp.concatenate([ma, mb], 2)
-    m_all = joined(core1, m_own, hop(m_own, "gcol", 1))
+    m_all = joined(core1, (ma, mb), (hop(ma, "gcol", 1), hop(mb, "gcol", 1)))
     acc = mixed((hh, hl), m_all)
 
-    h_parts, w_own, w_sib = [], [], []
+    h_parts, mine, others = [], [], []
     for k, q in enumerate(sums):
-        back = gb if k % 2 == 0 else up
+        back = backs[k]
         h_parts.append(halves(q, place[zb[0]], 0)[0])
         row = gather(q, place, zb, zb[1:], zb[:1]).reshape(Z, b, bc).transpose(1, 0, 2).reshape(b, half)
         w = turned(core1, row, hop(row, "gcol", 1), m_all)
-        w = gather(w, place, gb, back).reshape(G * b, half)
-        w_own.append(w)
-        w_sib.append(hop(w, "gcol", 1))
+        w = gather(w, place, gb, back[:-1]).reshape(G * b // 2, half)
+        got = hop(w, *back[-1])
+        mine.append((w, hop(w, "gcol", 1)))
+        others.append((got, hop(got, "gcol", 1)))
+
+    part = None
+    for j in range(2):
+        part = less(at, acc, (ph, pl_), [w[j] for w in mine], j == 1, False, part)
+    out = None
+    for j in range(2):
+        out = less(at, part, (ph, pl_), [w[j] for w in others], j == 1, True, out, True)
 
     h = jnp.concatenate(h_parts, 0)
     projected = lax.ppermute(h, "gcol", [(i, (i % 2) * Z + i // 2) for i in range(C)])
-    near = less(core1, acc, (ph, pl_), w_own)
-    return less(core1, acc, (ph, pl_), w_sib, near), projected
+    return out, projected
 
 
 def solution(mesh):

time: 146 us -> 139 us (0.952)
  the two profiles are of different devices: /device:TPU:8 before, /device:TPU:0 now
where the time goes in v3:
time: 139 us
  waiting for transfers between devices  58.1 us (42%)
  starting transfers between devices  39.5 us (28%)
  Pallas kernels  36.9 us (27%)
  other arithmetic  1.86 us (1%)
  local copies, waits for them, and re-layouts  1.7 us (1%)
    ppermute x30, waiting for transfers between devices, hop(): return lax.ppermute(x, axis, [(i, i ^ mask) for i in range(n)])  58.1 us
    ppermute x30, starting transfers between devices, hop(): return lax.ppermute(x, axis, [(i, i ^ mask) for i in range(n)])  38.5 us
    pallas_call x4, Pallas kernels, less(): pl.pallas_call(less_kernel, grid_spec=pltpu.PrefetchScalarGridSpec(num_sc...  14.2 us
    pallas_call x1, Pallas kernels, first(): pl.pallas_call(functools.partial(first_kernel, dims, masks), grid_spec=pl...  10 us
    pallas_call x1, Pallas kernels, mixed(): pl.pallas_call(mixed_kernel, grid=(rows // t,), in_specs=[blk, blk] + [pl...  6.84 us
    pallas_call x2, Pallas kernels, second(): pl.pallas_call(functools.partial(second_kernel, dims), grid_spec=pltpu.Pr...  3.61 us
  transfers between devices with their start and end apart: 31, of which 16 were waited for; matrix products, arithmetic and copies ran while one was open for 1% of the time, Pallas kernels for 16%

profile of v3, /device:TPU:0, one launch (start us, length us, event | category | flops | bytes accessed | tf_op | source)
XLA Modules:
  0.0 139.1 jit_solution(4082758986401543934)
XLA Ops:
  1.4 10.0 %first.1 = (f32[4,4,128,128]{3,2,1,0:T(8,128)S(1)}, f32[4,4,128,128]{3,2,1,0:T(8,128)S(1)}, bf16[2,2,1024,256]{3,2,1,0:T(8,128)(2,1)}, bf16[2,2,1024,256]{3,2,1,...) custom-call(s32[1]{0:T(128)} %bitcast.core_ref, ...), custom_call_target="tpu_custom_call" | custom-call | flops 3221225472 | bytes 12582912 | tf_op jit(solution)/shard_map/first/pallas_call | solution.py:96
  11.5 4.1 %collective-permute-start = (f32[256,128]{1,0:T(8,128)S(1)}, f32[256,128]{1,0:T(8,128)S(1)}, u32[]{:S(2)}, u32[]{:S(2)}) collective-permute-start(f32[256,128]{1,0:T(8,128)S(1)} %copy-done.3), channel_id=1, source_target_pairs={{0,4},{1,5},{2,6},{3,7},{4,0},{5,1},{6,2},{7,3},{8,12},{9,13},{10,... | collective-permute-start | bytes 393224 | tf_op jit(solution)/shard_map/ppermute | solution.py:272
  15.5 6.3 %collective-permute-done = f32[256,128]{1,0:T(8,128)S(1)} collective-permute-done((f32[256,128]{1,0:T(8,128)S(1)}, f32[256,128]{1,0:T(8,128)S(1)}, u32[]{:S(2)}, u32[]{:S(2)}) %collective-permute-start) | collective-permute-done | bytes 131104 | tf_op jit(solution)/shard_map/ppermute | solution.py:272
  23.2 6.2 %collective-permute-done.1 = f32[2,256,128]{2,1,0:T(8,128)S(1)} collective-permute-done((f32[2,256,128]{2,1,0:T(8,128)S(1)}, f32[2,256,128]{2,1,0:T(8,128)S(1)}, u32[]{:S(2)}, u32[]{:S(2)}) %collective-permute-start.1) | collective-permute-done | bytes 262176 | tf_op jit(solution)/shard_map/ppermute | solution.py:272
  37.6 6.1 %collective-permute-done.4 = f32[2,2,128,128]{3,2,0,1:T(8,128)S(1)} collective-permute-done((f32[2,2,128,128]{3,2,0,1:T(8,128)S(1)}, f32[2,2,128,128]{3,2,0,1:T(8,128)S(1)}, u32[]{:S(2)}, u32[]{:S(2)}) %collective-permute-start.4) | collective-permute-done | bytes 262176 | tf_op jit(solution)/shard_map/ppermute | solution.py:272
  48.2 6.8 %collective-permute-done.3 = f32[2,2,2,128,128]{4,3,1,2,0:T(8,128)S(1)} collective-permute-done((f32[2,2,2,128,128]{4,3,1,2,0:T(8,128)S(1)}, f32[2,2,2,128,128]{4,3,1,2,0:T(8,128)S(1)}, u32[]{:S(2)}, u32[]{:S(2)}) %collective-permute-start.3) | collective-permute-done | bytes 524320 | tf_op jit(solution)/shard_map/ppermute | solution.py:272
  55.0 2.5 %collective-permute-done.5 = f32[2,2,2,128,128]{4,3,1,2,0:T(8,128)S(1)} collective-permute-done((f32[2,2,2,128,128]{4,3,1,2,0:T(8,128)S(1)}, f32[2,2,2,128,128]{4,3,1,2,0:T(8,128)S(1)}, u32[]{:S(2)}, u32[]{:S(2)}) %collective-permute-start.5) | collective-permute-done | bytes 524320 | tf_op jit(solution)/shard_map/ppermute | solution.py:272
  58.7 4.7 %collective-permute-done.18 = f32[2,2,2,128,128]{4,3,1,2,0:T(8,128)S(1)} collective-permute-done((f32[2,2,2,128,128]{4,3,1,2,0:T(8,128)S(1)}, f32[2,2,2,128,128]{4,3,1,2,0:T(8,128)S(1)}, u32[]{:S(2)}, u32[]{:S(2)}) %collective-permute-start.18) | collective-permute-done | bytes 524320 | tf_op jit(solution)/shard_map/ppermute | solution.py:272
  65.7 4.1 %collective-permute-done.19 = f32[2,2,128,128]{3,2,0,1:T(8,128)S(1)} collective-permute-done((f32[2,2,128,128]{3,2,0,1:T(8,128)S(1)}, f32[2,2,128,128]{3,2,0,1:T(8,128)S(1)}, u32[]{:S(2)}, u32[]{:S(2)}) %collective-permute-start.19) | collective-permute-done | bytes 262176 | tf_op jit(solution)/shard_map/ppermute | solution.py:272
  69.9 2.5 %collective-permute-start.20 = (f32[2,128,128]{2,1,0:T(8,128)S(1)}, f32[2,128,128]{2,1,0:T(8,128)S(1)}, u32[]{:S(2)}, u32[]{:S(2)}) collective-permute-start(f32[2,128,128]{2,1,0:T(8,128)S(1)} %select_bitcast_fusion.19), channel_id=1, source_target_pairs={{0,2},{1,3},{2,0},{3,1},{4,6},{5,7},{6,4},{7,5},{8,10},{9,11},{10,... | collective-permute-start | bytes 393224 | tf_op jit(solution)/shard_map/ppermute | solution.py:272
  73.3 2.1 %collective-permute-done.20 = f32[2,128,128]{2,1,0:T(8,128)S(1)} collective-permute-done((f32[2,128,128]{2,1,0:T(8,128)S(1)}, f32[2,128,128]{2,1,0:T(8,128)S(1)}, u32[]{:S(2)}, u32[]{:S(2)}) %collective-permute-start.20) | collective-permute-done | bytes 131104 | tf_op jit(solution)/shard_map/ppermute | solution.py:272
  75.4 5.4 %collective-permute-start.21 = (f32[2,128,128]{2,1,0:T(8,128)S(1)}, f32[2,128,128]{2,1,0:T(8,128)S(1)}, u32[]{:S(2)}, u32[]{:S(2)}) collective-permute-start(f32[2,128,128]{2,1,0:T(8,128)S(1)} %bitcast_add_fusion.3), channel_id=1, source_target_pairs={{0,4},{1,5},{2,6},{3,7},{4,0},{5,1},{6,2},{7,3},{8,12},{9,13},{10,... | collective-permute-start | bytes 393224 | tf_op jit(solution)/shard_map/ppermute | solution.py:272
  80.9 2.4 %collective-permute-start.12 = (f32[2,128,128]{2,1,0:T(8,128)S(1)}, f32[2,128,128]{2,1,0:T(8,128)S(1)}, u32[]{:S(2)}, u32[]{:S(2)}) collective-permute-start(f32[2,128,128]{2,1,0:T(8,128)S(1)} %bitcast_add_fusion.4), channel_id=1, source_target_pairs={{0,4},{1,5},{2,6},{3,7},{4,0},{5,1},{6,2},{7,3},{8,12},{9,13},{10,... | collective-permute-start | bytes 393224 | tf_op jit(solution)/shard_map/ppermute | solution.py:272
  83.3 1.9 %collective-permute-done.21 = f32[2,128,128]{2,1,0:T(8,128)S(1)} collective-permute-done((f32[2,128,128]{2,1,0:T(8,128)S(1)}, f32[2,128,128]{2,1,0:T(8,128)S(1)}, u32[]{:S(2)}, u32[]{:S(2)}) %collective-permute-start.21) | collective-permute-done | bytes 131104 | tf_op jit(solution)/shard_map/ppermute | solution.py:272
  85.5 2.2 %collective-permute-done.12 = f32[2,128,128]{2,1,0:T(8,128)S(1)} collective-permute-done((f32[2,128,128]{2,1,0:T(8,128)S(1)}, f32[2,128,128]{2,1,0:T(8,128)S(1)}, u32[]{:S(2)}, u32[]{:S(2)}) %collective-permute-start.12) | collective-permute-done | bytes 131104 | tf_op jit(solution)/shard_map/ppermute | solution.py:272
  90.6 2.2 %collective-permute-done.13 = f32[2,128,128]{2,1,0:T(8,128)S(1)} collective-permute-done((f32[2,128,128]{2,1,0:T(8,128)S(1)}, f32[2,128,128]{2,1,0:T(8,128)S(1)}, u32[]{:S(2)}, u32[]{:S(2)}) %collective-permute-start.13) | collective-permute-done | bytes 131104 | tf_op jit(solution)/shard_map/ppermute | solution.py:272
  96.6 5.7 %collective-permute-done.24 = f32[128,512]{1,0:T(8,128)S(1)} collective-permute-done((f32[128,512]{1,0:T(8,128)S(1)}, f32[128,512]{1,0:T(8,128)S(1)}, u32[]{:S(2)}, u32[]{:S(2)}) %collective-permute-start.24) | collective-permute-done | bytes 262176 | tf_op jit(solution)/shard_map/ppermute | solution.py:272
  105.9 4.3 %collective-permute-start.25 = (f32[256,512]{1,0:T(8,128)S(1)}, f32[256,512]{1,0:T(8,128)S(1)}, u32[]{:S(2)}, u32[]{:S(2)}) collective-permute-start(f32[256,512]{1,0:T(8,128)S(1)} %bitcast.96), channel_id=1, source_target_pairs={{0,1},{1,0},{2,3},{3,2},{4,5},{5,4},{6,7},{7,6},{8,9},{9,8},{10,11... | collective-permute-start | bytes 1572872 | tf_op jit(solution)/shard_map/ppermute | solution.py:272
  110.4 5.6 %collective-permute-done.28.rest_5_ = f32[256,512]{1,0:T(8,128)S(1)} collective-permute-done((f32[256,512]{1,0:T(8,128)S(1)}, f32[256,512]{1,0:T(8,128)S(1)}, u32[]{:S(2)}, u32[]{:S(2)}) %collective-permute-start.28) | collective-permute-done | bytes 524320 | tf_op jit(solution)/shard_map/ppermute | solution.py:272
  117.3 6.8 %mixed.1.acc_ref = f32[1024,1024]{1,0:T(8,128)S(1)} custom-call(bf16[1024,1024]{1,0:T(8,128)(2,1)S(1)} %get-tuple-element.23.hh_ref, bf16[1024,1024]{1,0:T(8,128)(2,1)S(1)} %get-tuple-element.24.hl_ref, bf16[1024,1024]{1,0:T(8,128)(2,1)S(1)} %get-tuple-element.31.mh_ref.m1h.m2h, bf16[1024,1024]{1,0:T(8,128)(2,1)S(1)} %get-tuple-element.32.ml_ref.m1l.m2l), custom_call_target="tpu_custom_call" | custom-call | flops 6442450944 | bytes 16777216 | tf_op jit(solution)/shard_map/mixed/pallas_call | solution.py:187
  124.2 3.1 %less.4.rest_6_ = f32[1024,1024]{1,0:T(8,128)S(1)} custom-call(s32[3]{0:T(128)S(1)} %pad_add_fusion.at_ref, f32[1024,1024]{1,0:T(8,128)S(1)} %mixed.1.acc_ref, bf16[2,2,1024,256]{3,2,1,0:T(8,128)(2,1)S(1)} %copy-done, bf16[2,2,1024,256]{3,2,1,0:T(8,128)(2,1)S(1)} %copy-done, bf16[2,2,1024,256]{3,2,1,0:T(8,128)(2,1)S(1)} %copy-done.1, ...), custom_call_target="tpu_custom_call" | custom-call | flops 1610612736 | bytes 8388608 | tf_op jit(solution)/shard_map/less/pallas_call | solution.py:245
  127.4 3.1 %less.5.acc_ref = f32[1024,1024]{1,0:T(8,128)S(1)} custom-call(s32[3]{0:T(128)S(1)} %pad_add_fusion.at_ref, f32[1024,1024]{1,0:T(8,128)S(1)} %mixed.1.acc_ref, bf16[2,2,1024,256]{3,2,1,0:T(8,128)(2,1)S(1)} %copy-done, bf16[2,2,1024,256]{3,2,1,0:T(8,128)(2,1)S(1)} %copy-done, bf16[2,2,1024,256]{3,2,1,0:T(8,128)(2,1)S(1)} %copy-done.1, ...), custom_call_target="tpu_custom_call", output_to_operand_aliasing={{}: (8, {})} | custom-call | flops 1610612736 | bytes 8388608 | tf_op jit(solution)/shard_map/less/pallas_call | solution.py:245
  130.5 4.0 %less.6.rest_6_ = f32[1024,1024]{1,0:T(8,128)} custom-call(s32[3]{0:T(128)S(1)} %pad_add_fusion.at_ref, f32[1024,1024]{1,0:T(8,128)S(1)} %less.5.acc_ref, bf16[2,2,1024,256]{3,2,1,0:T(8,128)(2,1)S(1)} %copy-done, bf16[2,2,1024,256]{3,2,1,0:T(8,128)(2,1)S(1)} %copy-done, bf16[2,2,1024,256]{3,2,1,0:T(8,128)(2,1)S(1)} %copy-done.1, ...), custom_call_target="tpu_custom_call" | custom-call | flops 1610612736 | bytes 8388608 | tf_op jit(solution)/shard_map/less/pallas_call | solution.py:245
  134.5 4.0 %less.7 = f32[1024,1024]{1,0:T(8,128)} custom-call(s32[3]{0:T(128)S(1)} %pad_add_fusion.at_ref, f32[1024,1024]{1,0:T(8,128)S(1)} %less.5.acc_ref, bf16[2,2,1024,256]{3,2,1,0:T(8,128)(2,1)S(1)} %copy-done, bf16[2,2,1024,256]{3,2,1,0:T(8,128)(2,1)S(1)} %copy-done, bf16[2,2,1024,256]{3,2,1,0:T(8,128)(2,1)S(1)} %copy-done.1, ...), custom_call_target="tpu_custom_call", output_to_operand_aliasing={{}: (8, {})} | custom-call | flops 1610612736 | bytes 8388608 | tf_op jit(solution)/shard_map/less/pallas_call | solution.py:245
  (104 shorter events, 31.8 us)
Async XLA Ops:
  11.5 10.4 %collective-permute-start = (f32[256,128]{1,0:T(8,128)S(1)}, f32[256,128]{1,0:T(8,128)S(1)}, u32[]{:S(2)}, u32[]{:S(2)}) collective-permute-start(f32[256,128]{1,0:T(8,128)S(1)} %copy-done.3), channel_id=1, source_target_pairs={{0,4},{1,5},{2,6},{3,7},{4,0},{5,1},{6,2},{7,3},{8,12},{9,13},{10,... | collective-permute-start | bytes 393224 | tf_op jit(solution)/shard_map/ppermute | solution.py:272
  21.9 7.5 %collective-permute-start.1 = (f32[2,256,128]{2,1,0:T(8,128)S(1)}, f32[2,256,128]{2,1,0:T(8,128)S(1)}, u32[]{:S(2)}, u32[]{:S(2)}) collective-permute-start(f32[2,256,128]{2,1,0:T(8,128)S(1)} %pad_maximum_fusion.7), channel_id=1, source_target_pairs={{0,2},{1,3},{2,0},{3,1},{4,6},{5,7},{6,4},{7,5},{8,10},{9,11},{10,... | collective-permute-start | bytes 786440 | tf_op jit(solution)/shard_map/ppermute | solution.py:272
  22.7 23.7 %collective-permute-start.8 = (f32[4,4,128,128]{3,2,1,0:T(8,128)S(1)}, f32[4,4,128,128]{3,2,1,0:T(8,128)S(1)}, u32[]{:S(2)}, u32[]{:S(2)}) collective-permute-start(f32[4,4,128,128]{3,2,1,0:T(8,128)S(1)} %get-tuple-element.29), channel_id=1, source_target_pairs={{0,1},{1,0},{2,3},{3,2},{4,5},{5,4},{6,7},{7,6},{8,9},{9,8},{10,11... | collective-permute-start | bytes 3145736 | tf_op jit(solution)/shard_map/ppermute | solution.py:272
  22.7 22.0 %collective-permute-start.17 = (f32[4,4,128,128]{3,2,1,0:T(8,128)S(1)}, f32[4,4,128,128]{3,2,1,0:T(8,128)S(1)}, u32[]{:S(2)}, u32[]{:S(2)}) collective-permute-start(f32[4,4,128,128]{3,2,1,0:T(8,128)S(1)} %get-tuple-element.37), channel_id=1, source_target_pairs={{0,1},{1,0},{2,3},{3,2},{4,5},{5,4},{6,7},{7,6},{8,9},{9,8},{10,11... | collective-permute-start | bytes 3145736 | tf_op jit(solution)/shard_map/ppermute | solution.py:272
  34.5 9.2 %collective-permute-start.4 = (f32[2,2,128,128]{3,2,0,1:T(8,128)S(1)}, f32[2,2,128,128]{3,2,0,1:T(8,128)S(1)}, u32[]{:S(2)}, u32[]{:S(2)}) collective-permute-start(f32[2,2,128,128]{3,2,0,1:T(8,128)S(1)} %get-tuple-element.52), channel_id=1, source_target_pairs={{0,16},{8,24},{16,0},{24,8},{1,17},{9,25},{17,1},{25,9},{2,18},{10... | collective-permute-start | bytes 786440 | tf_op jit(solution)/shard_map/ppermute | solution.py:272
  36.3 18.7 %collective-permute-start.3 = (f32[2,2,2,128,128]{4,3,1,2,0:T(8,128)S(1)}, f32[2,2,2,128,128]{4,3,1,2,0:T(8,128)S(1)}, u32[]{:S(2)}, u32[]{:S(2)}) collective-permute-start(f32[2,2,2,128,128]{4,3,1,2,0:T(8,128)S(1)} %pad_maximum_fusion.2), channel_id=1, source_target_pairs={{0,16},{8,24},{16,0},{24,8},{1,17},{9,25},{17,1},{25,9},{2,18},{10... | collective-permute-start | bytes 1572872 | tf_op jit(solution)/shard_map/ppermute | solution.py:272
  43.9 13.6 %collective-permute-start.5 = (f32[2,2,2,128,128]{4,3,1,2,0:T(8,128)S(1)}, f32[2,2,2,128,128]{4,3,1,2,0:T(8,128)S(1)}, u32[]{:S(2)}, u32[]{:S(2)}) collective-permute-start(f32[2,2,2,128,128]{4,3,1,2,0:T(8,128)S(1)} %pad_maximum_fusion.3), channel_id=1, source_target_pairs={{0,8},{8,0},{16,24},{24,16},{1,9},{9,1},{17,25},{25,17},{2,10},{10... | collective-permute-start | bytes 1572872 | tf_op jit(solution)/shard_map/ppermute | solution.py:272
  44.9 18.4 %collective-permute-start.18 = (f32[2,2,2,128,128]{4,3,1,2,0:T(8,128)S(1)}, f32[2,2,2,128,128]{4,3,1,2,0:T(8,128)S(1)}, u32[]{:S(2)}, u32[]{:S(2)}) collective-permute-start(f32[2,2,2,128,128]{4,3,1,2,0:T(8,128)S(1)} %copy.20), channel_id=1, source_target_pairs={{0,16},{8,24},{16,0},{24,8},{1,17},{9,25},{17,1},{25,9},{2,18},{10... | collective-permute-start | bytes 1572872 | tf_op jit(solution)/shard_map/ppermute | solution.py:272
  46.6 17.6 %collective-permute-start.9 = (f32[2,2,2,128,128]{4,3,1,2,0:T(8,128)S(1)}, f32[2,2,2,128,128]{4,3,1,2,0:T(8,128)S(1)}, u32[]{:S(2)}, u32[]{:S(2)}) collective-permute-start(f32[2,2,2,128,128]{4,3,1,2,0:T(8,128)S(1)} %select_bitcast_fusion), channel_id=1, source_target_pairs={{0,8},{8,0},{16,24},{24,16},{1,9},{9,1},{17,25},{25,17},{2,10},{10... | collective-permute-start | bytes 1572872 | tf_op jit(solution)/shard_map/ppermute | solution.py:272
  57.8 31.5 %collective-permute-start.7 = (f32[4,4,128,128]{3,2,1,0:T(8,128)S(1)}, f32[4,4,128,128]{3,2,1,0:T(8,128)S(1)}, u32[]{:S(2)}, u32[]{:S(2)}) collective-permute-start(f32[4,4,128,128]{3,2,1,0:T(8,128)S(1)} %bitcast.91), channel_id=1, source_target_pairs={{0,1},{1,0},{2,3},{3,2},{4,5},{5,4},{6,7},{7,6},{8,9},{9,8},{10,11... | collective-permute-start | bytes 3145736 | tf_op jit(solution)/shard_map/ppermute | solution.py:272
  58.1 31.3 %collective-permute-start.6 = (f32[4,4,128,128]{3,2,1,0:T(8,128)S(1)}, f32[4,4,128,128]{3,2,1,0:T(8,128)S(1)}, u32[]{:S(2)}, u32[]{:S(2)}) collective-permute-start(f32[4,4,128,128]{3,2,1,0:T(8,128)S(1)} %bitcast.93), channel_id=1, source_target_pairs={{0,1},{1,0},{2,3},{3,2},{4,5},{5,4},{6,7},{7,6},{8,9},{9,8},{10,11... | collective-permute-start | bytes 3145736 | tf_op jit(solution)/shard_map/ppermute | solution.py:272
  64.4 8.1 %collective-permute-start.10 = (f32[2,2,128,128]{3,2,0,1:T(8,128)S(1)}, f32[2,2,128,128]{3,2,0,1:T(8,128)S(1)}, u32[]{:S(2)}, u32[]{:S(2)}) collective-permute-start(f32[2,2,128,128]{3,2,0,1:T(8,128)S(1)} %select_bitcast_fusion.10), channel_id=1, source_target_pairs={{0,16},{8,24},{16,0},{24,8},{1,17},{9,25},{17,1},{25,9},{2,18},{10... | collective-permute-start | bytes 786440 | tf_op jit(solution)/shard_map/ppermute | solution.py:272
  72.5 8.3 %collective-permute-start.11 = (f32[2,128,128]{2,1,0:T(8,128)S(1)}, f32[2,128,128]{2,1,0:T(8,128)S(1)}, u32[]{:S(2)}, u32[]{:S(2)}) collective-permute-start(f32[2,128,128]{2,1,0:T(8,128)S(1)} %select_bitcast_fusion.22), channel_id=1, source_target_pairs={{0,2},{1,3},{2,0},{3,1},{4,6},{5,7},{6,4},{7,5},{8,10},{9,11},{10,... | collective-permute-start | bytes 393224 | tf_op jit(solution)/shard_map/ppermute | solution.py:272
  75.4 9.8 %collective-permute-start.21 = (f32[2,128,128]{2,1,0:T(8,128)S(1)}, f32[2,128,128]{2,1,0:T(8,128)S(1)}, u32[]{:S(2)}, u32[]{:S(2)}) collective-permute-start(f32[2,128,128]{2,1,0:T(8,128)S(1)} %bitcast_add_fusion.3), channel_id=1, source_target_pairs={{0,4},{1,5},{2,6},{3,7},{4,0},{5,1},{6,2},{7,3},{8,12},{9,13},{10,... | collective-permute-start | bytes 393224 | tf_op jit(solution)/shard_map/ppermute | solution.py:272
  80.9 6.8 %collective-permute-start.12 = (f32[2,128,128]{2,1,0:T(8,128)S(1)}, f32[2,128,128]{2,1,0:T(8,128)S(1)}, u32[]{:S(2)}, u32[]{:S(2)}) collective-permute-start(f32[2,128,128]{2,1,0:T(8,128)S(1)} %bitcast_add_fusion.4), channel_id=1, source_target_pairs={{0,4},{1,5},{2,6},{3,7},{4,0},{5,1},{6,2},{7,3},{8,12},{9,13},{10,... | collective-permute-start | bytes 393224 | tf_op jit(solution)/shard_map/ppermute | solution.py:272
  93.5 8.8 %collective-permute-start.24 = (f32[128,512]{1,0:T(8,128)S(1)}, f32[128,512]{1,0:T(8,128)S(1)}, u32[]{:S(2)}, u32[]{:S(2)}) collective-permute-start(f32[128,512]{1,0:T(8,128)S(1)} %turned.3), channel_id=1, source_target_pairs={{0,8},{8,0},{16,24},{24,16},{1,9},{9,1},{17,25},{25,17},{2,10},{10... | collective-permute-start | bytes 786440 | tf_op jit(solution)/shard_map/ppermute | solution.py:272
  95.0 9.0 %collective-permute-start.15 = (f32[128,512]{1,0:T(8,128)S(1)}, f32[128,512]{1,0:T(8,128)S(1)}, u32[]{:S(2)}, u32[]{:S(2)}) collective-permute-start(f32[128,512]{1,0:T(8,128)S(1)} %turned.2), channel_id=1, source_target_pairs={{0,16},{8,24},{16,0},{24,8},{1,17},{9,25},{17,1},{25,9},{2,18},{10... | collective-permute-start | bytes 786440 | tf_op jit(solution)/shard_map/ppermute | solution.py:272
  102.4 13.5 %collective-permute-start.28 = (f32[256,512]{1,0:T(8,128)S(1)}, f32[256,512]{1,0:T(8,128)S(1)}, u32[]{:S(2)}, u32[]{:S(2)}) collective-permute-start(f32[256,512]{1,0:T(8,128)S(1)} %bitcast.95), channel_id=1, source_target_pairs={{0,16},{8,24},{16,0},{24,8},{1,17},{9,25},{17,1},{25,9},{2,18},{10... | collective-permute-start | bytes 1572872 | tf_op jit(solution)/shard_map/ppermute | solution.py:272
  104.1 13.3 %collective-permute-start.26 = (f32[256,512]{1,0:T(8,128)S(1)}, f32[256,512]{1,0:T(8,128)S(1)}, u32[]{:S(2)}, u32[]{:S(2)}) collective-permute-start(f32[256,512]{1,0:T(8,128)S(1)} %bitcast.98), channel_id=1, source_target_pairs={{0,8},{8,0},{16,24},{24,16},{1,9},{9,1},{17,25},{25,17},{2,10},{10... | collective-permute-start | bytes 1572872 | tf_op jit(solution)/shard_map/ppermute | solution.py:272
  105.0 19.2 %collective-permute-start.30 = (f32[256,128]{1,0:T(8,128)S(1)}, f32[256,128]{1,0:T(8,128)S(1)}, u32[]{:S(2)}, u32[]{:S(2)}) collective-permute-start(f32[256,128]{1,0:T(8,128)S(1)} %pad_maximum_fusion.10), channel_id=1, source_target_pairs={{0,0},{1,4},{2,1},{3,5},{4,2},{5,6},{6,3},{7,7},{8,8},{9,12},{10,9... | collective-permute-start | bytes 393224 | tf_op jit(solution)/shard_map/ppermute | solution.py:362
  105.9 21.4 %collective-permute-start.25 = (f32[256,512]{1,0:T(8,128)S(1)}, f32[256,512]{1,0:T(8,128)S(1)}, u32[]{:S(2)}, u32[]{:S(2)}) collective-permute-start(f32[256,512]{1,0:T(8,128)S(1)} %bitcast.96), channel_id=1, source_target_pairs={{0,1},{1,0},{2,3},{3,2},{4,5},{5,4},{6,7},{7,6},{8,9},{9,8},{10,11... | collective-permute-start | bytes 1572872 | tf_op jit(solution)/shard_map/ppermute | solution.py:272
  110.3 17.1 %collective-permute-start.16 = (f32[256,512]{1,0:T(8,128)S(1)}, f32[256,512]{1,0:T(8,128)S(1)}, u32[]{:S(2)}, u32[]{:S(2)}) collective-permute-start(f32[256,512]{1,0:T(8,128)S(1)} %bitcast.99), channel_id=1, source_target_pairs={{0,1},{1,0},{2,3},{3,2},{4,5},{5,4},{6,7},{7,6},{8,9},{9,8},{10,11... | collective-permute-start | bytes 1572872 | tf_op jit(solution)/shard_map/ppermute | solution.py:272
  115.9 18.6 %collective-permute-start.29 = (f32[256,512]{1,0:T(8,128)S(1)}, f32[256,512]{1,0:T(8,128)S(1)}, u32[]{:S(2)}, u32[]{:S(2)}) collective-permute-start(f32[256,512]{1,0:T(8,128)S(1)} %collective-permute-done.28.rest_5_), channel_id=1, source_target_pairs={{0,1},{1,0},{2,3},{3,2},{4,5},{5,4},{6,7},{7,6},{8,9},{9,8},{10,11... | collective-permute-start | bytes 1572872 | tf_op jit(solution)/shard_map/ppermute | solution.py:272
  117.3 17.2 %collective-permute-start.27 = (f32[256,512]{1,0:T(8,128)S(1)}, f32[256,512]{1,0:T(8,128)S(1)}, u32[]{:S(2)}, u32[]{:S(2)}) collective-permute-start(f32[256,512]{1,0:T(8,128)S(1)} %collective-permute-done.26.rest_4_), channel_id=1, source_target_pairs={{0,1},{1,0},{2,3},{3,2},{4,5},{5,4},{6,7},{7,6},{8,9},{9,8},{10,11... | collective-permute-start | bytes 1572872 | tf_op jit(solution)/shard_map/ppermute | solution.py:272
  (11 other events, 82.1 us)
